TPU v7x, 256 devices: a whole 4x4x8 slice. The times are simulated.
256 devices in a mesh: rep: 32 (over z, y), data: 8 (over x, core).
Axes of the slice: x: 4, y: 4, z: 8, core: 2. Of those that a mesh axis runs over, the one named last changes fastest.
Arguments:
- w1: bfloat16 [2, 1536, 6144], replicated
- w2: bfloat16 [2, 6144, 1536], replicated
- x: bfloat16 [768, 1, 64, 1536], P(('rep', 'data'))
- dy: bfloat16 [768, 1, 64, 1536], P(('rep', 'data'))
Outputs:
- output 1: bfloat16 [2, 1536, 6144], replicated
- output 2: bfloat16 [2, 6144, 1536], replicated
- output 3: bfloat16 [768, 1, 64, 1536], P(('rep', 'data'))
All inputs are finite; a program needn't handle non-finite values.
Results may differ from a plain program's by a relative error of at most 0.02.
Values are sent between devices in bfloat16 or wider.
A program may use at most 768 MiB of HBM per device.

v0:
```python
import jax
import jax.numpy as jnp
from jax import lax
from jax.sharding import PartitionSpec as P

GC = 0.7978845608028654
GA = 0.044715
AXES = ("rep", "data")


def gelu_pair(u):
    t = jnp.tanh(GC * (u + GA * u * u * u))
    val = 0.5 * u * (1.0 + t)
    der = 0.5 * (1.0 + t) + 0.5 * u * (1.0 - t * t) * GC * (1.0 + 3.0 * GA * u * u)
    return val, der


def solution(mesh):
    ndev = mesh.shape["rep"] * mesh.shape["data"]

    def local(w1, w2, x, dy):
        nl, nd, ff = w1.shape
        nb, ns = x.shape[1], x.shape[2]
        tok = nb * ns
        fs = ff // ndev

        def step(carry, inp):
            s1, s2 = carry
            xm, gm = inp
            h = xm.reshape(tok, nd)
            g = gm.reshape(tok, nd)
            hs, us, acts = [], [], []
            for l in range(nl):
                u = jnp.dot(h, w1[l], preferred_element_type=jnp.float32).astype(jnp.bfloat16)
                act = gelu_pair(u.astype(jnp.float32))[0].astype(jnp.bfloat16)
                hs.append(h)
                us.append(u)
                acts.append(act)
                if l + 1 < nl:
                    h = (h.astype(jnp.float32) + jnp.dot(act, w2[l], preferred_element_type=jnp.float32)).astype(jnp.bfloat16)
            d1 = [None] * nl
            d2 = [None] * nl
            for l in reversed(range(nl)):
                da = jnp.dot(g, w2[l].T, preferred_element_type=jnp.float32)
                du = (da * gelu_pair(us[l].astype(jnp.float32))[1]).astype(jnp.bfloat16)
                d2[l] = jnp.dot(acts[l].T, g, preferred_element_type=jnp.float32)
                d1[l] = jnp.dot(hs[l].T, du, preferred_element_type=jnp.float32)
                g = (g.astype(jnp.float32) + jnp.dot(du, w1[l].T, preferred_element_type=jnp.float32)).astype(jnp.bfloat16)
            n1 = [s1[l] + lax.psum_scatter(d1[l].astype(jnp.bfloat16), AXES, scatter_dimension=1, tiled=True).astype(jnp.float32) for l in range(nl)]
            n2 = [s2[l] + lax.psum_scatter(d2[l].astype(jnp.bfloat16), AXES, scatter_dimension=0, tiled=True).astype(jnp.float32) for l in range(nl)]
            return (tuple(n1), tuple(n2)), g.reshape(nb, ns, nd)

        init = (tuple(jnp.zeros((nd, fs), jnp.float32) for l in range(nl)), tuple(jnp.zeros((fs, nd), jnp.float32) for l in range(nl)))
        (s1, s2), dx = lax.scan(step, init, (x, dy))
        g1 = jnp.stack([lax.all_gather(s.astype(jnp.bfloat16), AXES, axis=1, tiled=True) for s in s1])
        g2 = jnp.stack([lax.all_gather(s.astype(jnp.bfloat16), AXES, axis=0, tiled=True) for s in s2])
        return g1, g2, dx

    return jax.shard_map(local, mesh=mesh, in_specs=(P(), P(), P(AXES), P(AXES)), out_specs=(P(), P(), P(AXES)), check_vma=False)
```

profile of v0, /device:TPU:1, one launch (start us, length us, event | category | flops | bytes accessed | tf_op | source)
XLA Modules:
  0.0 6009.8 jit_solution(4036734548595452230)
XLA Ops:
  8.0 5447.5 %while.19 = (s32[]{:T(128)}, f32[1536,24]{0,1:T(8,128)}, f32[1536,24]{0,1:T(8,128)}, f32[24,1536]{1,0:T(8,128)S(1)}, f32[24,1536]{1,0:T(8,128)S(1)}, /*index=5*/...) while((s32[]{:T(128)}, f32[1536,24]{0,1:T(8,128)}, ...), condition=%wide.region_5.6_spmd.clone, body=%wide.region_0.5_spmd.clone.sunk | while | flops 13353762816 | bytes 462815840 | solution.py:54
  43.3 13.0 fusion.156
  97.8 10.5 convolution_convert_fusion.8
  118.7 382.3 %reduce-scatter.9.cloned.1.call-done = bf16[24,1536]{1,0:T(8,128)(2,1)} async-done(((bf16[6144,1536]{1,0:T(8,128)(2,1)}), bf16[24,1536]{1,0:T(8,128)(2,1)}) %reduce-scatter.9.cloned.1.call-update) | async-done | bytes 73744 | tf_op jit(solution)/shard_map/while/body/eval_jaxpr/reduce_scatter | solution.py:50
  501.9 439.3 %reduce-scatter.11.cloned.1.call-done = bf16[24,1536]{1,0:T(8,128)(2,1)} async-done(((bf16[6144,1536]{1,0:T(8,128)(2,1)}), bf16[24,1536]{1,0:T(8,128)(2,1)}) %reduce-scatter.11.cloned.1.call-update) | async-done | bytes 73744 | tf_op jit(solution)/shard_map/while/body/eval_jaxpr/reduce_scatter | solution.py:50
  942.2 439.9 %reduce-scatter.7.cloned.1.call-done = bf16[1536,24]{0,1:T(8,128)(2,1)} async-done(((bf16[1536,6144]{0,1:T(8,128)(2,1)}), bf16[1536,24]{0,1:T(8,128)(2,1)}) %reduce-scatter.7.cloned.1.call-update) | async-done | bytes 73744 | tf_op jit(solution)/shard_map/while/body/eval_jaxpr/reduce_scatter | solution.py:49
  1383.0 439.8 %reduce-scatter.5.cloned.1.call-done = bf16[1536,24]{0,1:T(8,128)(2,1)} async-done(((bf16[1536,6144]{0,1:T(8,128)(2,1)}), bf16[1536,24]{0,1:T(8,128)(2,1)}) %reduce-scatter.5.cloned.1.call-update) | async-done | bytes 73744 | tf_op jit(solution)/shard_map/while/body/eval_jaxpr/reduce_scatter | solution.py:49
  1859.5 13.0 fusion.156
  1934.9 381.8 %reduce-scatter.9.cloned.1.call-done = bf16[24,1536]{1,0:T(8,128)(2,1)} async-done(((bf16[6144,1536]{1,0:T(8,128)(2,1)}), bf16[24,1536]{1,0:T(8,128)(2,1)}) %reduce-scatter.9.cloned.1.call-update) | async-done | bytes 73744 | tf_op jit(solution)/shard_map/while/body/eval_jaxpr/reduce_scatter | solution.py:50
  2317.7 439.3 %reduce-scatter.11.cloned.1.call-done = bf16[24,1536]{1,0:T(8,128)(2,1)} async-done(((bf16[6144,1536]{1,0:T(8,128)(2,1)}), bf16[24,1536]{1,0:T(8,128)(2,1)}) %reduce-scatter.11.cloned.1.call-update) | async-done | bytes 73744 | tf_op jit(solution)/shard_map/while/body/eval_jaxpr/reduce_scatter | solution.py:50
  2757.9 439.8 %reduce-scatter.7.cloned.1.call-done = bf16[1536,24]{0,1:T(8,128)(2,1)} async-done(((bf16[1536,6144]{0,1:T(8,128)(2,1)}), bf16[1536,24]{0,1:T(8,128)(2,1)}) %reduce-scatter.7.cloned.1.call-update) | async-done | bytes 73744 | tf_op jit(solution)/shard_map/while/body/eval_jaxpr/reduce_scatter | solution.py:49
  3198.7 440.0 %reduce-scatter.5.cloned.1.call-done = bf16[1536,24]{0,1:T(8,128)(2,1)} async-done(((bf16[1536,6144]{0,1:T(8,128)(2,1)}), bf16[1536,24]{0,1:T(8,128)(2,1)}) %reduce-scatter.5.cloned.1.call-update) | async-done | bytes 73744 | tf_op jit(solution)/shard_map/while/body/eval_jaxpr/reduce_scatter | solution.py:49
  3675.4 13.0 fusion.156
  3750.8 381.8 %reduce-scatter.9.cloned.1.call-done = bf16[24,1536]{1,0:T(8,128)(2,1)} async-done(((bf16[6144,1536]{1,0:T(8,128)(2,1)}), bf16[24,1536]{1,0:T(8,128)(2,1)}) %reduce-scatter.9.cloned.1.call-update) | async-done | bytes 73744 | tf_op jit(solution)/shard_map/while/body/eval_jaxpr/reduce_scatter | solution.py:50
  4133.6 439.1 %reduce-scatter.11.cloned.1.call-done = bf16[24,1536]{1,0:T(8,128)(2,1)} async-done(((bf16[6144,1536]{1,0:T(8,128)(2,1)}), bf16[24,1536]{1,0:T(8,128)(2,1)}) %reduce-scatter.11.cloned.1.call-update) | async-done | bytes 73744 | tf_op jit(solution)/shard_map/while/body/eval_jaxpr/reduce_scatter | solution.py:50
  4573.6 439.8 %reduce-scatter.7.cloned.1.call-done = bf16[1536,24]{0,1:T(8,128)(2,1)} async-done(((bf16[1536,6144]{0,1:T(8,128)(2,1)}), bf16[1536,24]{0,1:T(8,128)(2,1)}) %reduce-scatter.7.cloned.1.call-update) | async-done | bytes 73744 | tf_op jit(solution)/shard_map/while/body/eval_jaxpr/reduce_scatter | solution.py:49
  5014.4 439.6 %reduce-scatter.5.cloned.1.call-done = bf16[1536,24]{0,1:T(8,128)(2,1)} async-done(((bf16[1536,6144]{0,1:T(8,128)(2,1)}), bf16[1536,24]{0,1:T(8,128)(2,1)}) %reduce-scatter.5.cloned.1.call-update) | async-done | bytes 73744 | tf_op jit(solution)/shard_map/while/body/eval_jaxpr/reduce_scatter | solution.py:49
  5460.2 131.1 %all-gather.5.cloned.1.call-done = bf16[1536,6144]{0,1:T(8,128)(2,1)} async-done(((bf16[1536,24]{0,1:T(8,128)(2,1)}), bf16[1536,6144]{0,1:T(8,128)(2,1)}) %all-gather.5.cloned.1.call-update) | async-done | bytes 18874384 | tf_op jit(solution)/shard_map/all_gather | solution.py:55
  5591.3 128.7 %all-gather.7.cloned.1.call-done = bf16[1536,6144]{0,1:T(8,128)(2,1)} async-done(((bf16[1536,24]{0,1:T(8,128)(2,1)}), bf16[1536,6144]{0,1:T(8,128)(2,1)}) %all-gather.7.cloned.1.call-update) | async-done | bytes 18874384 | tf_op jit(solution)/shard_map/all_gather | solution.py:55
  5720.0 25.7 pad_maximum_fusion
  5745.7 48.6 copy.9
  5794.3 53.9 all-gather.9.cloned.1.call-done
  5848.2 128.3 %all-gather.11.cloned.1.call-done = bf16[6144,1536]{1,0:T(8,128)(2,1)} async-done(((bf16[24,1536]{1,0:T(8,128)(2,1)}), bf16[6144,1536]{1,0:T(8,128)(2,1)}) %all-gather.11.cloned.1.call-update) | async-done | bytes 18874384 | tf_op jit(solution)/shard_map/all_gather | solution.py:56
  5976.5 25.7 pad_maximum_fusion.1
  (130 shorter events, 299.5 us)
Async XLA Ops:
  8.1 492.9 %reduce-scatter.9.cloned.1.call-start = ((), (), s32[]{:S(2)}) async-start(), calls=%async_computation.10 | async-start | bytes 18948096 | tf_op jit(solution)/shard_map/while/body/eval_jaxpr/reduce_scatter | solution.py:50
  66.4 874.8 %reduce-scatter.11.cloned.1.call-start = ((), (), s32[]{:S(2)}) async-start(), calls=%async_computation.11 | async-start | bytes 18948096 | tf_op jit(solution)/shard_map/while/body/eval_jaxpr/reduce_scatter | solution.py:50
  76.6 1305.5 %reduce-scatter.7.cloned.1.call-start = ((), (), s32[]{:S(2)}) async-start(), calls=%async_computation.9 | async-start | bytes 18948096 | tf_op jit(solution)/shard_map/while/body/eval_jaxpr/reduce_scatter | solution.py:49
  87.2 1735.5 %reduce-scatter.5.cloned.1.call-start = ((), (), s32[]{:S(2)}) async-start(), calls=%async_computation.8 | async-start | bytes 18948096 | tf_op jit(solution)/shard_map/while/body/eval_jaxpr/reduce_scatter | solution.py:49
  108.3 1273.8 %copy-start.1 = (f32[1536,24]{0,1:T(8,128)S(1)}, f32[1536,24]{0,1:T(8,128)}, u32[]{:S(2)}) copy-start(f32[1536,24]{0,1:T(8,128)} %get-tuple-element.195) | copy-start | bytes 442372 | tf_op jit(solution)/shard_map/while
  108.3 1714.5 %copy-start.3 = (f32[1536,24]{0,1:T(8,128)S(1)}, f32[1536,24]{0,1:T(8,128)}, u32[]{:S(2)}) copy-start(f32[1536,24]{0,1:T(8,128)} %get-tuple-element.194) | copy-start | bytes 442372 | tf_op jit(solution)/shard_map/while
  1383.0 440.7 %copy-start.2 = (f32[1536,24]{0,1:T(8,128)}, f32[1536,24]{0,1:T(8,128)S(1)}, u32[]{:S(2)}) copy-start(f32[1536,24]{0,1:T(8,128)S(1)} %select_add_fusion.9) | copy-start | bytes 442372 | tf_op jit(solution)/shard_map/while
  1824.3 492.4 %reduce-scatter.9.cloned.1.call-start = ((), (), s32[]{:S(2)}) async-start(), calls=%async_computation.10 | async-start | bytes 18948096 | tf_op jit(solution)/shard_map/while/body/eval_jaxpr/reduce_scatter | solution.py:50
  1882.6 874.3 %reduce-scatter.11.cloned.1.call-start = ((), (), s32[]{:S(2)}) async-start(), calls=%async_computation.11 | async-start | bytes 18948096 | tf_op jit(solution)/shard_map/while/body/eval_jaxpr/reduce_scatter | solution.py:50
  1892.8 1304.9 %reduce-scatter.7.cloned.1.call-start = ((), (), s32[]{:S(2)}) async-start(), calls=%async_computation.9 | async-start | bytes 18948096 | tf_op jit(solution)/shard_map/while/body/eval_jaxpr/reduce_scatter | solution.py:49
  1903.5 1735.2 %reduce-scatter.5.cloned.1.call-start = ((), (), s32[]{:S(2)}) async-start(), calls=%async_computation.8 | async-start | bytes 18948096 | tf_op jit(solution)/shard_map/while/body/eval_jaxpr/reduce_scatter | solution.py:49
  1924.5 1273.2 %copy-start.1 = (f32[1536,24]{0,1:T(8,128)S(1)}, f32[1536,24]{0,1:T(8,128)}, u32[]{:S(2)}) copy-start(f32[1536,24]{0,1:T(8,128)} %get-tuple-element.195) | copy-start | bytes 442372 | tf_op jit(solution)/shard_map/while
  1924.5 1714.2 %copy-start.3 = (f32[1536,24]{0,1:T(8,128)S(1)}, f32[1536,24]{0,1:T(8,128)}, u32[]{:S(2)}) copy-start(f32[1536,24]{0,1:T(8,128)} %get-tuple-element.194) | copy-start | bytes 442372 | tf_op jit(solution)/shard_map/while
  3198.6 441.0 %copy-start.2 = (f32[1536,24]{0,1:T(8,128)}, f32[1536,24]{0,1:T(8,128)S(1)}, u32[]{:S(2)}) copy-start(f32[1536,24]{0,1:T(8,128)S(1)} %select_add_fusion.9) | copy-start | bytes 442372 | tf_op jit(solution)/shard_map/while
  3640.3 492.4 %reduce-scatter.9.cloned.1.call-start = ((), (), s32[]{:S(2)}) async-start(), calls=%async_computation.10 | async-start | bytes 18948096 | tf_op jit(solution)/shard_map/while/body/eval_jaxpr/reduce_scatter | solution.py:50
  3698.5 874.1 %reduce-scatter.11.cloned.1.call-start = ((), (), s32[]{:S(2)}) async-start(), calls=%async_computation.11 | async-start | bytes 18948096 | tf_op jit(solution)/shard_map/while/body/eval_jaxpr/reduce_scatter | solution.py:50
  3708.7 1304.7 %reduce-scatter.7.cloned.1.call-start = ((), (), s32[]{:S(2)}) async-start(), calls=%async_computation.9 | async-start | bytes 18948096 | tf_op jit(solution)/shard_map/while/body/eval_jaxpr/reduce_scatter | solution.py:49
  3719.4 1734.6 %reduce-scatter.5.cloned.1.call-start = ((), (), s32[]{:S(2)}) async-start(), calls=%async_computation.8 | async-start | bytes 18948096 | tf_op jit(solution)/shard_map/while/body/eval_jaxpr/reduce_scatter | solution.py:49
  3740.4 1273.0 %copy-start.1 = (f32[1536,24]{0,1:T(8,128)S(1)}, f32[1536,24]{0,1:T(8,128)}, u32[]{:S(2)}) copy-start(f32[1536,24]{0,1:T(8,128)} %get-tuple-element.195) | copy-start | bytes 442372 | tf_op jit(solution)/shard_map/while
  3740.4 1713.6 %copy-start.3 = (f32[1536,24]{0,1:T(8,128)S(1)}, f32[1536,24]{0,1:T(8,128)}, u32[]{:S(2)}) copy-start(f32[1536,24]{0,1:T(8,128)} %get-tuple-element.194) | copy-start | bytes 442372 | tf_op jit(solution)/shard_map/while
  5455.6 135.8 %all-gather.5.cloned.1.call-start = ((), (), s32[]{:S(2)}) async-start(), calls=%async_computation.4 | async-start | bytes 18948096 | tf_op jit(solution)/shard_map/all_gather | solution.py:55
  5457.1 262.9 %all-gather.7.cloned.1.call-start = ((), (), s32[]{:S(2)}) async-start(), calls=%async_computation.5 | async-start | bytes 18948096 | tf_op jit(solution)/shard_map/all_gather | solution.py:55
  5458.8 389.4 %all-gather.9.cloned.1.call-start = ((), (), s32[]{:S(2)}) async-start(), calls=%async_computation.6 | async-start | bytes 18948096 | tf_op jit(solution)/shard_map/all_gather | solution.py:56
  5459.5 517.0 %all-gather.11.cloned.1.call-start = ((), (), s32[]{:S(2)}) async-start(), calls=%async_computation.7 | async-start | bytes 18948096 | tf_op jit(solution)/shard_map/all_gather | solution.py:56
  (16 other events, 477.1 us)
Sparse Core Ops, SparseCore 0:
  66.5 434.4 reduce-scatter.8
  507.4 433.7 reduce-scatter.10
  948.2 433.7 reduce-scatter.6
  1388.9 433.8 reduce-scatter.4
  1882.7 433.9 reduce-scatter.8
  2323.0 433.8 reduce-scatter.10
  2763.9 433.7 reduce-scatter.6
  3204.7 433.9 reduce-scatter.4
  3698.6 433.9 reduce-scatter.8
  4138.9 433.6 reduce-scatter.10
  4579.7 433.7 reduce-scatter.6
  5020.3 433.6 reduce-scatter.4
Sparse Core Ops, SparseCore 1:
  5460.4 130.9 all-gather.4
  5595.5 124.5 all-gather.6
  5723.7 124.5 all-gather.8
  5852.0 124.5 all-gather.10
where the time goes:
time: 6010 us
  waiting for transfers between devices  5540 us (92%)
  matrix products  325 us (5%)
  other arithmetic  66.9 us (1%)
    reduce_scatter x6, waiting for transfers between devices, step(): lax.psum_scatter(d1[l].astype(jnp.bfloat16), AXES, scatter_dimension=1, t...  2640 us
    reduce_scatter x6, waiting for transfers between devices, step(): lax.psum_scatter(d2[l].astype(jnp.bfloat16), AXES, scatter_dimension=0, t...  2460 us
    all_gather x2, waiting for transfers between devices, local(): lax.all_gather(s.astype(jnp.bfloat16), AXES, axis=1, tiled=True)  260 us
    all_gather x2, waiting for transfers between devices, local(): lax.all_gather(s.astype(jnp.bfloat16), AXES, axis=0, tiled=True)  182 us
  transfers between devices with their start and end apart: 16, of which 16 were waited for; matrix products, arithmetic and copies ran while one was open for 4% of the time, Pallas kernels for 0%

commit v1 on v0

v1 whole, which is shorter than its diff:
```python
import functools

import jax
import jax.numpy as jnp
from jax import lax
from jax.experimental import pallas as pl
from jax.experimental.pallas import tpu as pltpu
from jax.sharding import PartitionSpec as P

GC = 0.7978845608028654
GA = 0.044715
AXES = ("rep", "data")
MESH = pl.DeviceIdType.MESH
BF16 = jnp.bfloat16
F32 = jnp.float32

UR, UC = 48, 128
TR = 384
COLOURS = 3
ORDERS = (("x", "y", "z"), ("y", "x", "z"), ("z", "x", "y"))
SUB = 8
NSL = 4
OFF_RS = (1, 2, 3)
OFF_AG = (6, 5, 4)
TICKS = 11


def gelu_pair(u):
    t = jnp.tanh(GC * (u + GA * u * u * u))
    val = 0.5 * u * (1.0 + t)
    der = 0.5 * (1.0 + t) + 0.5 * u * (1.0 - t * t) * GC * (1.0 + 3.0 * GA * u * u)
    return val, der


def sub_of(n, i):
    if n == 8:
        return max(0, i - 1)
    return (0, 1, 3)[i] if n == 4 else 1


class Comm:
    def __init__(self, sizes, ff, d, tok):
        self.sizes, self.ff, self.d, self.tok = sizes, ff, d, tok
        self.units = ff // UR * 2
        self.tiles = ff // TR
        self.tu = TR // UR * 2
        self.cw = d // 2 // COLOURS
        self.n = [[sizes[a] for a in o] for o in ORDERS]
        self.stride, self.off, total = [], [], 0
        for c in range(COLOURS):
            s, st, of = self.units, [], []
            for f in range(3):
                s //= self.n[c][f]
                st.append(s)
                of.append(total)
                total += self.n[c][f] - 1
            self.stride.append(st)
            self.off.append(of)
        self.total = total

    def slot_shapes(self):
        return [
            pltpu.VMEM((2, self.n[c][f] - 1, self.stride[c][f] // 2, UR, UC), BF16)
            for c in range(COLOURS)
            for f in range(3)
        ]


def half_of(direction, i):
    return i % 2 if direction == 0 else 1 - i % 2


def comm_kernel(cm, *refs):
    srcs = refs[: 2 * NSL]
    out = refs[2 * NSL]
    g, lr, lt, stage = refs[2 * NSL + 1 : 2 * NSL + 5]
    slots = refs[2 * NSL + 5 : 2 * NSL + 14]
    (rs_ss, rs_rs, ag_ss, ag_rs, rs_c1, rs_c2, ag_c1, ag_c2, x_ss, x_rs, ld, p_ss, p_rs, o_s) = refs[2 * NSL + 14 :]
    nx, ny, nz = cm.sizes["x"], cm.sizes["y"], cm.sizes["z"]
    rep = lax.axis_index("rep")
    dat = lax.axis_index("data")
    pos = {"z": rep // ny, "y": rep % ny, "x": dat // 2}
    core = dat % 2

    def device(dim, step):
        p = dict(pos)
        n = cm.sizes[dim]
        p[dim] = (pos[dim] + step + n) % n
        return {"rep": p["z"] * ny + p["y"], "data": p["x"] * 2 + core}

    nbr = {(a, s): device(a, s) for a in ("x", "y", "z") for s in (1, -1)}
    partner = {"rep": rep, "data": pos["x"] * 2 + (1 - core)}

    def neighbour(c, f, direction):
        return nbr[(ORDERS[c][f], 1 if direction == 0 else -1)]

    def sender(c, f, direction):
        return nbr[(ORDERS[c][f], -1 if direction == 0 else 1)]

    bases = []
    for c in range(COLOURS):
        b, bs = 0, []
        for f in range(3):
            bs.append(b)
            b = b + pos[ORDERS[c][f]] * cm.stride[c][f]
        bases.append(bs)

    def region(c, f, step, half):
        n, s = cm.n[c][f], cm.stride[c][f]
        owner = (pos[ORDERS[c][f]] + step + n) % n
        return bases[c][f] + owner * s + half * (s // 2)

    def rs_region(c, f, direction, i):
        k = cm.n[c][f] // 2 - (i + 1) // 2
        return region(c, f, k if direction == 0 else -k, half_of(direction, i))

    def ag_region(c, f, direction, i):
        k = i // 2
        return region(c, f, -k if direction == 0 else k, half_of(direction, i))

    def rs_copy(c, f, direction, i, q):
        h = cm.stride[c][f] // 2
        j = cm.off[c][f] + i
        return pltpu.make_async_remote_copy(
            src_ref=g.at[q, c, pl.ds(rs_region(c, f, direction, i), h)],
            dst_ref=slots[3 * c + f].at[direction, i],
            send_sem=rs_ss.at[direction, j],
            recv_sem=rs_rs.at[direction, j],
            device_id=neighbour(c, f, direction),
            device_id_type=MESH,
        )

    def ag_copy(c, f, direction, i, q):
        h = cm.stride[c][f] // 2
        j = cm.off[c][f] + i
        ref = g.at[q, c, pl.ds(ag_region(c, f, direction, i), h)]
        return pltpu.make_async_remote_copy(
            src_ref=ref,
            dst_ref=ref,
            send_sem=ag_ss.at[direction, j],
            recv_sem=ag_rs.at[direction, j],
            device_id=neighbour(c, f, direction),
            device_id_type=MESH,
        )

    def push(c, start, count, q):
        ref = g.at[q, c, pl.ds(start, count)]
        there = out.at[q, core, c, pl.ds(start, count)]
        pltpu.make_async_remote_copy(
            src_ref=ref, dst_ref=there, send_sem=p_ss.at[q, c], recv_sem=p_rs.at[q, c], device_id=partner, device_id_type=MESH
        ).start()
        pltpu.make_async_copy(ref, there, o_s.at[q, c]).start()

    def signal(sem, dev):
        pl.semaphore_signal(sem, inc=1, device_id=dev, device_id_type=MESH)

    def sem3(ref, c, f, direction):
        return ref.at[3 * c + f, direction]

    def add_units(c, start, h, parts, q):
        b = min(8, h)

        def one(j, carry):
            at = start + j * b
            v = g[q, c, pl.ds(at, b)].astype(F32)
            for slot, direction, m in parts:
                v = v + slot[direction, m, pl.ds(j * b, b)].astype(F32)
            g[q, c, pl.ds(at, b)] = v.astype(BF16)
            return carry

        if h == b:
            one(0, 0)
        else:
            lax.fori_loop(0, h // b, one, 0)

    def rs_step(c, f, i, q):
        n, h = cm.n[c][f], cm.stride[c][f] // 2
        for direction in (0, 1):
            if i >= 2:
                rs_copy(c, f, direction, i - 2, q).wait_recv()
                add_units(c, rs_region(c, f, direction, i), h, [(slots[3 * c + f], direction, i - 2)], q)

            @pl.when(q >= 1)
            def _():
                if i == 0 and n >= 4:
                    pl.semaphore_wait(sem3(rs_c1, c, f, direction), 1)
                if i == max(n - 3, 0):
                    pl.semaphore_wait(sem3(rs_c2, c, f, direction), 1)

            rs_copy(c, f, direction, i, q).start()

    def ag_step(c, f, i, q):
        n, h = cm.n[c][f], cm.stride[c][f] // 2
        if f == 0 and i == 0:
            push(c, region(c, f, 0, 0), 2 * h, q)
        for direction in (0, 1):
            if i >= 2:
                ag_copy(c, f, direction, i - 2, q).wait_recv()
            if i == 0:
                pl.semaphore_wait(sem3(ag_c1, c, f, direction), 1)
            if i == max(n - 3, 0):

                @pl.when(q >= 1)
                def _():
                    pl.semaphore_wait(sem3(ag_c2, c, f, direction), 1)

            ag_copy(c, f, direction, i, q).start()
            if f == 0 and i >= 2:
                push(c, ag_region(c, f, direction, i), h, q)

    def early_sends(c, f, q, copy):
        for i in range(min(2, cm.n[c][f] - 1)):
            for direction in (0, 1):
                copy(c, f, direction, i, q).wait_send()

    def late_sends(c, f, q, copy):
        for i in range(2, cm.n[c][f] - 1):
            for direction in (0, 1):
                copy(c, f, direction, i, q).wait_send()

    def rs_fin(c, f, q):
        n, h = cm.n[c][f], cm.stride[c][f] // 2
        parts = ([], [])
        for m in range(max(n - 3, 0), n - 1):
            for direction in (0, 1):
                rs_copy(c, f, direction, m, q).wait_recv()
                parts[half_of(direction, m)].append((slots[3 * c + f], direction, m))
        for half in (0, 1):
            add_units(c, region(c, f, 0, half), h, parts[half], q)
        late_sends(c, f, q, rs_copy)

        @pl.when(q < NSL - 1)
        def _():
            for direction in (0, 1):
                signal(sem3(rs_c2, c, f, direction), sender(c, f, direction))

    def ag_fin(c, f, q):
        n, h = cm.n[c][f], cm.stride[c][f] // 2
        for m in range(max(n - 3, 0), n - 1):
            for direction in (0, 1):
                ag_copy(c, f, direction, m, q).wait_recv()
                if f == 0:
                    k = m // 2 + 1
                    push(c, region(c, f, -k if direction == 0 else k, half_of(direction, m)), h, q)
        late_sends(c, f, q, ag_copy)

        @pl.when(q < NSL - 1)
        def _():
            for direction in (0, 1):
                signal(sem3(ag_c2, c, f, direction), sender(c, f, direction))

    def load(q, par):
        return (
            pltpu.make_async_copy(srcs[2 * q], lr.at[par, :, pl.ds(0, cm.ff)], ld.at[par, 0]),
            pltpu.make_async_copy(srcs[2 * q + 1], lr.at[par, :, pl.ds(cm.ff, cm.d)], ld.at[par, 1]),
        )

    jt = cm.d // TR

    def compute(q, s):
        par = q % 2
        odd = q % 2

        def rows(tau):
            return pl.multiple_of((1 - odd) * tau * TR + odd * (cm.ff + (tau % jt) * TR), UC)

        def cols(tau, k, c):
            return pl.multiple_of((1 - odd) * cm.ff + odd * (tau // jt) * cm.d + k * (cm.d // 2) + c * cm.cw, UC)

        def x_copy(tau):
            return pltpu.make_async_remote_copy(
                src_ref=stage.at[tau % 2],
                dst_ref=g.at[q, :, pl.ds(tau * cm.tu, cm.tu)],
                send_sem=x_ss.at[tau % 2],
                recv_sem=x_rs.at[tau],
                device_id=partner,
                device_id_type=MESH,
            )

        def product(tau, k, c):
            r = lr[par, :, pl.ds(cols(tau, k, c), cm.cw)]
            return jnp.dot(lt[tau % 2], r, preferred_element_type=F32)

        def tile(t, carry):
            @pl.when(t < cm.tiles)
            def _():
                lt[t % 2] = lr[par, :, pl.ds(rows(t), TR)].T

                @pl.when(t >= 2)
                def _():
                    x_copy(t - 2).wait_send()

                def colour(c, carry):
                    v = product(t, 1 - core, c).astype(BF16)
                    for u in range(cm.tu):
                        stage[t % 2, c, u] = v[u // 2 * UR : u // 2 * UR + UR, u % 2 * UC : u % 2 * UC + UC]
                    return carry

                lax.fori_loop(0, COLOURS, colour, 0)
                x_copy(t).start()

            @pl.when(t >= 1)
            def _():
                tau = t - 1
                x_copy(tau).wait_recv()

                def colour(c, carry):
                    v = product(tau, core, c)
                    for u in range(cm.tu):
                        w = v[u // 2 * UR : u // 2 * UR + UR, u % 2 * UC : u % 2 * UC + UC]
                        w = w + g[q, c, tau * cm.tu + u].astype(F32)
                        g[q, c, tau * cm.tu + u] = w.astype(BF16)
                    return carry

                lax.fori_loop(0, COLOURS, colour, 0)

            return carry

        total = cm.tiles + 1
        lax.fori_loop(s * total // SUB, (s + 1) * total // SUB, tile, 0)
        if s == SUB - 1:
            for t in (cm.tiles - 2, cm.tiles - 1):
                x_copy(t).wait_send()

    barrier = pltpu.get_barrier_semaphore()
    peers = list(nbr.values()) + [partner]
    for dev in peers:
        signal(barrier, dev)
    for cp in load(0, 0):
        cp.start()
    pl.semaphore_wait(barrier, len(peers))

    def active(t, off):
        return (t >= off) & (t < off + NSL)

    def each(fn, f, q, cond=None):
        for c in range(COLOURS):
            fn(c, f, q)

    def steps(fn, f, s, q, only=None):
        for c in range(COLOURS):
            n = cm.n[c][f]
            for i in range(n - 1):
                if sub_of(n, i) == s:
                    fn(c, f, i, q)

    def tick(t, carry):
        for s in range(SUB):
            if s == 0:
                for q in range(1, NSL):

                    @pl.when(t + 1 == q)
                    def _(q=q):
                        for cp in load(q, q % 2):
                            cp.start()

                @pl.when(active(t, 0))
                def _():
                    for cp in load(0, t % 2):
                        cp.wait()

            for fn, f, off in ((rs_step, 0, OFF_RS[0]), (ag_step, 0, OFF_AG[0])):

                @pl.when(active(t, off))
                def _(fn=fn, f=f, off=off):
                    steps(fn, f, s, t - off)

            for fn, f, off in ((rs_step, 2, OFF_RS[2]), (ag_step, 2, OFF_AG[2]), (ag_step, 1, OFF_AG[1])):

                @pl.when(active(t, off))
                def _(fn=fn, f=f, off=off):
                    steps(fn, f, s, t - off)

            if s == 0:

                @pl.when(active(t, OFF_AG[0] + 1))
                def _():
                    each(ag_fin, 0, t - OFF_AG[0] - 1)

                @pl.when(active(t, OFF_RS[0] + 1))
                def _():
                    each(rs_fin, 0, t - OFF_RS[0] - 1)

            @pl.when(active(t, OFF_RS[1]))
            def _():
                steps(rs_step, 1, s, t - OFF_RS[1])

            @pl.when(active(t, 0))
            def _():
                compute(t, s)

            if s == SUB - 2:
                for f in range(3):

                    @pl.when(active(t, OFF_RS[f]))
                    def _(f=f):
                        q = t - OFF_RS[f]
                        for c in range(COLOURS):
                            early_sends(c, f, q, rs_copy)
                            if cm.n[c][f] >= 4:

                                @pl.when(q < NSL - 1)
                                def _(c=c):
                                    for direction in (0, 1):
                                        signal(sem3(rs_c1, c, f, direction), sender(c, f, direction))

                    @pl.when(active(t, OFF_AG[f]))
                    def _(f=f):
                        for c in range(COLOURS):
                            early_sends(c, f, t - OFF_AG[f], ag_copy)

            if s == SUB - 1:
                for f in (1, 2):

                    @pl.when(active(t, OFF_RS[f]))
                    def _(f=f):
                        each(rs_fin, f, t - OFF_RS[f])

                    @pl.when(active(t, OFF_AG[f]))
                    def _(f=f):
                        each(ag_fin, f, t - OFF_AG[f])

                for f in range(3):

                    @pl.when(active(t + 1, OFF_AG[f]))
                    def _(f=f):
                        for c in range(COLOURS):
                            for direction in (0, 1):
                                signal(sem3(ag_c1, c, f, direction), sender(c, f, direction))

        return carry

    lax.fori_loop(0, TICKS, tick, 0)
    for q in range(NSL):
        for c in range(COLOURS):
            cp = pltpu.make_async_remote_copy(
                src_ref=g.at[q, c],
                dst_ref=out.at[q, 1 - core, c],
                send_sem=p_ss.at[q, c],
                recv_sem=p_rs.at[q, c],
                device_id=partner,
                device_id_type=MESH,
            )
            cp.wait_send()
            cp.wait_recv()
            pltpu.make_async_copy(g.at[q, c], out.at[q, core, c], o_s.at[q, c]).wait()


def reduce_all(sizes, ff, d, tok, pieces):
    cm = Comm(sizes, ff, d, tok)
    dma = pltpu.SemaphoreType.DMA
    reg = pltpu.SemaphoreType.REGULAR
    any_spec = pl.BlockSpec(memory_space=pl.ANY)
    return pl.pallas_call(
        functools.partial(comm_kernel, cm),
        name="grad_sum",
        out_shape=jax.ShapeDtypeStruct((NSL, 2, COLOURS, cm.units, UR, UC), BF16),
        in_specs=[any_spec] * (2 * NSL),
        out_specs=any_spec,
        scratch_shapes=[
            pltpu.VMEM((NSL, COLOURS, cm.units, UR, UC), BF16),
            pltpu.VMEM((2, tok, ff + d), BF16),
            pltpu.VMEM((2, TR, tok), BF16),
            pltpu.VMEM((2, COLOURS, cm.tu, UR, UC), BF16),
        ]
        + cm.slot_shapes()
        + [dma((2, cm.total))] * 4
        + [reg((9, 2))] * 4
        + [dma((2,)), dma((cm.tiles,)), dma((2, 2))]
        + [dma((NSL, COLOURS))] * 3,
        compiler_params=pltpu.CompilerParams(collective_id=0, has_side_effects=True, vmem_limit_bytes=66_000_000),
        cost_estimate=pl.CostEstimate(flops=16 * tok * ff * d // 2, bytes_accessed=8 * ff * d, transcendentals=0),
    )(*pieces)


def place_kernel(tu, cw, o_ref, g_ref):
    for k in range(2):
        for c in range(COLOURS):
            for u in range(tu):
                at = k * COLOURS * cw + c * cw + u % 2 * UC
                g_ref[0, u // 2 * UR : u // 2 * UR + UR, at : at + UC] = o_ref[0, k, c, u]


def place(o, shape, q0, where):
    ff, d = max(shape[1:]), min(shape[1:])
    tu, cw = TR // UR * 2, d // 2 // COLOURS
    return pl.pallas_call(
        functools.partial(place_kernel, tu, cw),
        name="place",
        out_shape=jax.ShapeDtypeStruct(shape, BF16),
        grid=(shape[0], ff // TR),
        in_specs=[pl.BlockSpec((1, 2, COLOURS, tu, UR, UC), lambda l, t: (q0 - 2 * l, 0, 0, t, 0, 0))],
        out_specs=pl.BlockSpec((1, TR, d), where),
        compiler_params=pltpu.CompilerParams(dimension_semantics=("arbitrary", "arbitrary")),
        cost_estimate=pl.CostEstimate(flops=0, bytes_accessed=8 * ff * d, transcendentals=0),
    )(o)


def solution(mesh, sizes=None):
    if sizes is None:
        rep, data = mesh.shape["rep"], mesh.shape["data"]
        sizes = {"x": data // 2, "y": 4, "z": rep // 4}

    def local(w1, w2, x, dy):
        nl, nd, ff = w1.shape
        tok = x.shape[0] * x.shape[1] * x.shape[2]

        def mm(a, b):
            return jnp.dot(a, b, preferred_element_type=F32)

        h = x.reshape(tok, nd)
        g = dy.reshape(tok, nd)
        hs, us, acts = [], [], []
        for l in range(nl):
            u = mm(h, w1[l]).astype(BF16)
            act = gelu_pair(u.astype(F32))[0].astype(BF16)
            hs.append(h)
            us.append(u)
            acts.append(act)
            if l + 1 < nl:
                h = (h.astype(F32) + mm(act, w2[l])).astype(BF16)
        pieces = []
        for l in reversed(range(nl)):
            da = mm(g, w2[l].T)
            du = (da * gelu_pair(us[l].astype(F32))[1]).astype(BF16)
            pieces += [acts[l], g, du, hs[l]]
            g = (g.astype(F32) + mm(du, w1[l].T)).astype(BF16)
        o = reduce_all(sizes, ff, nd, tok, pieces)
        jt = nd // TR
        g1 = place(o, w1.shape, 3, lambda l, t: (l, t % jt, t // jt))
        g2 = place(o, w2.shape, 2, lambda l, t: (l, t, 0))
        return g1, g2, g.reshape(x.shape)

    return jax.shard_map(local, mesh=mesh, in_specs=(P(), P(), P(AXES), P(AXES)), out_specs=(P(), P(), P(AXES)), check_vma=False)
```

time: 6010 us -> 516 us (0.09)
  waiting for transfers between devices: 5540 us -> 0 us
  Pallas kernels: 0 us -> 438 us
  matrix products: 325 us -> 75.3 us
  other arithmetic: 66.9 us -> 0 us
    reduce_scatter x12 -> x0, waiting for transfers between devices: 5100 us -> none  [the longest x6 2640 us: step(): lax.psum_scatter(d1[l].astype(jnp.bfloat16), AXES, scatter_dimension=1, t...]
    all_gather x4 -> x0, waiting for transfers between devices: 442 us -> none  [the longest x2 260 us: local(): lax.all_gather(s.astype(jnp.bfloat16), AXES, axis=1, tiled=True)]
    pallas_call x0 -> x3, Pallas kernels: none -> 438 us  [the longest x1 361 us: reduce_all(): pl.pallas_call(functools.partial(comm_kernel, cm), name='grad_sum', out_s...]
    dot_general x33 -> x7, matrix products: 325 us -> 75.3 us  [mm(): return jnp.dot(a, b, preferred_element_type=F32)]
  transfers between devices with their start and end apart: 16 -> 0, of which waited for: 16 -> 0; matrix products, arithmetic and copies ran while one was open for 4% -> 0% of each run, Pallas kernels for 0% -> 0%
where the time goes in v1:
time: 516 us; the launch traced here: 514 us
  Pallas kernels  438 us (85%)
  matrix products  75.3 us (15%)
    pallas_call x1, Pallas kernels, reduce_all(): pl.pallas_call(functools.partial(comm_kernel, cm), name='grad_sum', out_s...  361 us
    pallas_call x2, Pallas kernels, place(): pl.pallas_call(functools.partial(place_kernel, tu, cw), name='place', out...  77 us
    dot_general x7, matrix products, mm(): return jnp.dot(a, b, preferred_element_type=F32)  75.3 us

profile of v1, /device:TPU:1, one launch (start us, length us, event | category | flops | bytes accessed | tf_op | source)
XLA Modules:
  0.0 514.2 jit_solution(16916033350631254955)
XLA Ops:
  0.6 0.0 copy-start.2
  0.6 10.2 %fusion.47 = (bf16[192,6144]{1,0:T(8,128)(2,1)}, bf16[192,6144]{1,0:T(8,128)(2,1)S(1)}) fusion(bf16[192,1536]{1,0:T(8,128)(2,1)} %bitcast.57, bf16[2,1536,6144]{2,1,0:T(8,128)(2,1)} %param.4), kind=kOutput, calls=%fused_computation.49 | convolution fusion | flops 3636854784 | bytes 24182784 | tf_op jit(solution)/shard_map/dot_general | solution.py:509
  10.9 0.0 copy-done.2
  10.9 8.9 %fusion.69.refs_3_ = bf16[192,1536]{1,0:T(8,128)(2,1)S(1)} fusion(bf16[2,6144,1536]{2,1,0:T(8,128)(2,1)} %param.5, bf16[192,1536]{1,0:T(8,128)(2,1)S(1)} %bitcast.59, bf16[192,6144]{1,0:T(8,128)(2,1)S(1)} %get-tuple-element.9), kind=kOutput, calls=%fused_computation.63 | convolution fusion | flops 3636559872 | bytes 22413312 | tf_op jit(solution)/shard_map/dot_general | solution.py:509
  19.7 0.0 copy-start.4
  19.7 0.0 copy-start.3
  19.7 10.4 %fusion.43 = (bf16[192,6144]{1,0:T(8,128)(2,1)}, bf16[192,6144]{1,0:T(8,128)(2,1)S(1)}) fusion(bf16[192,1536]{1,0:T(8,128)(2,1)S(1)} %fusion.69.refs_3_, bf16[2,1536,6144]{2,1,0:T(8,128)(2,1)} %param.4), kind=kOutput, calls=%fused_computation.45 | convolution fusion | flops 3636854784 | bytes 24182784 | tf_op jit(solution)/shard_map/dot_general | solution.py:509
  30.1 0.0 copy-done.4
  30.1 0.0 copy-done.3
  30.1 11.4 %fusion.27.refs_2_ = bf16[192,6144]{1,0:T(8,128)(2,1)S(1)} fusion(bf16[192,1536]{1,0:T(8,128)(2,1)S(1)} %bitcast.61, bf16[2,6144,1536]{2,1,0:T(8,128)(2,1)} %param.5, bf16[192,6144]{1,0:T(8,128)(2,1)S(1)} %get-tuple-element.7), kind=kOutput, calls=%fused_computation.37 | convolution fusion | flops 3647471616 | bytes 24182784 | tf_op jit(solution)/shard_map/dot_general | solution.py:509
  41.5 0.0 copy-start
  41.5 11.1 %fusion.66.refs_5_ = bf16[192,1536]{1,0:T(8,128)(2,1)S(1)} fusion(bf16[192,6144]{1,0:T(8,128)(2,1)S(1)} %fusion.27.refs_2_, bf16[2,1536,6144]{2,1,0:T(8,128)(2,1)} %param.4, bf16[192,1536]{1,0:T(8,128)(2,1)S(1)} %bitcast.62), kind=kOutput, calls=%fused_computation.62 | convolution fusion | flops 3624763392 | bytes 22413312 | tf_op jit(solution)/shard_map/dot_general | solution.py:509
  52.6 0.0 copy-done
  52.6 0.0 copy-start.5
  52.6 11.6 %fusion.30.refs_6_ = bf16[192,6144]{1,0:T(8,128)(2,1)S(1)} fusion(bf16[192,1536]{1,0:T(8,128)(2,1)S(1)} %fusion.66.refs_5_, bf16[2,6144,1536]{2,1,0:T(8,128)(2,1)} %param.5, bf16[192,6144]{1,0:T(8,128)(2,1)S(1)} %get-tuple-element.9), kind=kOutput, calls=%fused_computation.38 | convolution fusion | flops 3647471616 | bytes 24182784 | tf_op jit(solution)/shard_map/dot_general | solution.py:509
  64.3 0.0 copy-done.5
  64.3 0.0 copy-start.1
  64.3 11.8 %fusion.72 = bf16[192,1536]{1,0:T(8,128)(2,1)} fusion(bf16[192,6144]{1,0:T(8,128)(2,1)S(1)} %fusion.30.refs_6_, bf16[2,1536,6144]{2,1,0:T(8,128)(2,1)} %param.4, bf16[192,1536]{1,0:T(8,128)(2,1)S(1)} %fusion.66.refs_5_), kind=kOutput, calls=%fused_computation.64 | convolution fusion | flops 3624763392 | bytes 22413312 | tf_op jit(solution)/shard_map/dot_general | solution.py:509
  76.1 0.0 copy-done.1
  76.1 361.1 %grad_sum.1.o_ref = bf16[4,2,3,256,48,128]{5,4,3,2,1,0:T(8,128)(2,1)} custom-call(bf16[192,6144]{1,0:T(8,128)(2,1)} %get-tuple-element.6.refs_0_, bf16[192,1536]{1,0:T(8,128)(2,1)} %bitcast.60, bf16[192,6144]{1,0:T(8,128)(2,1)} %copy-done, bf16[192,1536]{1,0:T(8,128)(2,1)} %copy-done.4, bf16[192,6144]{1,0:T(8,128)(2,1)} %get-tuple-element.8.refs_4_, ...), custom_call_target="tpu_custom_call" | custom-call | flops 14495514624 | bytes 75497472 | tf_op jit(solution)/shard_map/grad_sum/pallas_call | solution.py:454
  437.2 38.5 %place.3 = bf16[2,6144,1536]{2,1,0:T(8,128)(2,1)} custom-call(bf16[4,2,3,256,48,128]{5,4,3,2,1,0:T(8,128)(2,1)} %grad_sum.1.o_ref), custom_call_target="tpu_custom_call" | custom-call | bytes 75497472 | tf_op jit(solution)/shard_map/place/pallas_call | solution.py:487
  475.7 38.5 %place.2 = bf16[2,1536,6144]{2,1,0:T(8,128)(2,1)} custom-call(bf16[4,2,3,256,48,128]{5,4,3,2,1,0:T(8,128)(2,1)} %grad_sum.1.o_ref), custom_call_target="tpu_custom_call" | custom-call | bytes 75497472 | tf_op jit(solution)/shard_map/place/pallas_call | solution.py:487
Async XLA Ops:
  0.6 10.2 %copy-start.2 = (bf16[3,1,64,1536]{3,2,1,0:T(8,128)(2,1)S(1)}, bf16[3,1,64,1536]{3,2,1,0:T(8,128)(2,1)}, u32[]{:S(2)}) copy-start(bf16[3,1,64,1536]{3,2,1,0:T(8,128)(2,1)} %param.6) | copy-start | bytes 1769476
  19.7 10.4 %copy-start.4 = (bf16[192,1536]{1,0:T(8,128)(2,1)}, bf16[192,1536]{1,0:T(8,128)(2,1)S(1)}, u32[]{:S(2)}) copy-start(bf16[192,1536]{1,0:T(8,128)(2,1)S(1)} %fusion.69.refs_3_) | copy-start | bytes 1769476
  19.7 10.4 %copy-start.3 = (bf16[3,1,64,1536]{3,2,1,0:T(8,128)(2,1)S(1)}, bf16[3,1,64,1536]{3,2,1,0:T(8,128)(2,1)}, u32[]{:S(2)}) copy-start(bf16[3,1,64,1536]{3,2,1,0:T(8,128)(2,1)} %param.7) | copy-start | bytes 1769476
  41.5 11.1 %copy-start = (bf16[192,6144]{1,0:T(8,128)(2,1)}, bf16[192,6144]{1,0:T(8,128)(2,1)S(1)}, u32[]{:S(2)}) copy-start(bf16[192,6144]{1,0:T(8,128)(2,1)S(1)} %fusion.27.refs_2_) | copy-start | bytes 7077892
  52.6 11.6 %copy-start.5 = (bf16[192,1536]{1,0:T(8,128)(2,1)}, bf16[192,1536]{1,0:T(8,128)(2,1)S(1)}, u32[]{:S(2)}) copy-start(bf16[192,1536]{1,0:T(8,128)(2,1)S(1)} %fusion.66.refs_5_) | copy-start | bytes 1769476
  64.3 11.8 %copy-start.1 = (bf16[192,6144]{1,0:T(8,128)(2,1)}, bf16[192,6144]{1,0:T(8,128)(2,1)S(1)}, u32[]{:S(2)}) copy-start(bf16[192,6144]{1,0:T(8,128)(2,1)S(1)} %fusion.30.refs_6_) | copy-start | bytes 7077892

commit v2 on v1

--- a/solution.py
+++ b/solution.py
@@ -20,9 +20,55 @@
 ORDERS = (("x", "y", "z"), ("y", "x", "z"), ("z", "x", "y"))
 SUB = 8
 NSL = 4
-OFF_RS = (1, 2, 3)
-OFF_AG = (6, 5, 4)
-TICKS = 11
+OFF_DW = 0
+OFF = {("rs", 0): 1, ("rs", 1): 2, ("rs", 2): 3, ("ag", 2): 4, ("ag", 1): 5, ("ag", 0): 6}
+SEND = {
+    ("rs", 0): {8: (0, 1, 2, 2, 3, 6, 7), 4: (0, 2, 4), 2: (1,)},
+    ("rs", 1): {8: (-1, 6, 11, 9, 8, 6, 10), 4: (0, 0, 2), 2: (1,)},
+    ("rs", 2): {8: (-1, 0, 1, 1, 2, 2, 5), 4: (1, 3, 4), 2: (1,)},
+    ("ag", 2): {8: (0, 1, 2, 2, 3, 4, 5), 4: (0, 0, 4), 2: (1,)},
+    ("ag", 1): {8: (1, -1, -2, 8, 2, 5, 8), 4: (-1, 0, 1), 2: (1,)},
+    ("ag", 0): {8: (0, 0, 1, 2, 3, 6, 6), 4: (-2, 2, 3), 2: (1,)},
+}
+FIN = {("rs", 0): 8, ("rs", 1): 7, ("rs", 2): 7, ("ag", 2): 7, ("ag", 1): 5, ("ag", 0): 8}
+EARLY = {("rs", 0): 6, ("rs", 1): 7, ("rs", 2): 7, ("ag", 2): 7, ("ag", 1): 3, ("ag", 0): 4}
+CREDIT = {("rs", 0): 7, ("rs", 1): 5, ("rs", 2): 6, ("ag", 2): -1, ("ag", 1): -4, ("ag", 0): -2}
+RANK = {
+    "load": 0,
+    ("send", "ag", 1): 1,
+    ("early", "ag", 2): 2,
+    ("send", "ag", 2): 3,
+    ("send", "rs", 2): 4,
+    ("send", "rs", 0): 5,
+    ("send", "ag", 0): 6,
+    ("fin", "ag", 2): 7,
+    ("early", "rs", 1): 8,
+    "chain": 9,
+    ("fin", "rs", 1): 10,
+    ("fin", "ag", 1): 11,
+    ("credit", "ag", 1): 12,
+    ("early", "ag", 1): 13,
+    ("early", "ag", 0): 14,
+    ("credit", "ag", 0): 15,
+    ("fin", "rs", 0): 16,
+    ("fin", "ag", 0): 17,
+    ("early", "rs", 2): 18,
+    ("credit", "rs", 1): 19,
+    ("credit", "rs", 0): 20,
+    ("fin", "rs", 2): 21,
+    "dw": 22,
+    ("send", "rs", 1): 24,
+    ("credit", "rs", 2): 25,
+    ("early", "rs", 0): 26,
+    ("credit", "ag", 2): 27,
+}
+LATE = 23
+CHAIN = {0: (0, 5), 1: (5, 12)}
+DW = {1: (0, 1), 2: (1, 7), 3: (7, 9), 5: (9, 11), 6: (11, 16), 7: (16, 18)}
+KT = 512
+WB = 3
+XB = 3
+LAG = 2
 
 
 def gelu_pair(u):
@@ -30,12 +76,6 @@
     val = 0.5 * u * (1.0 + t)
     der = 0.5 * (1.0 + t) + 0.5 * u * (1.0 - t * t) * GC * (1.0 + 3.0 * GA * u * u)
     return val, der
-
-
-def sub_of(n, i):
-    if n == 8:
-        return max(0, i - 1)
-    return (0, 1, 3)[i] if n == 4 else 1
 
 
 class Comm:
@@ -71,11 +111,9 @@
 
 
 def comm_kernel(cm, *refs):
-    srcs = refs[: 2 * NSL]
-    out = refs[2 * NSL]
-    g, lr, lt, stage = refs[2 * NSL + 1 : 2 * NSL + 5]
-    slots = refs[2 * NSL + 5 : 2 * NSL + 14]
-    (rs_ss, rs_rs, ag_ss, ag_rs, rs_c1, rs_c2, ag_c1, ag_c2, x_ss, x_rs, ld, p_ss, p_rs, o_s) = refs[2 * NSL + 14 :]
+    x_in, dy_in, h1_in, a1_in, a0_in, u1_in, u0_in, w1, w2, g, out, dx_out, lr, lt, stage, wb, ub, acc = refs[:18]
+    slots = refs[18:27]
+    (rs_ss, rs_rs, ag_ss, ag_rs, rs_c1, rs_c2, ag_c1, ag_c2, x_ss, x_rs, ld, p_ss, p_rs, w_s, u_s, d_s) = refs[27:]
     nx, ny, nz = cm.sizes["x"], cm.sizes["y"], cm.sizes["z"]
     rep = lax.axis_index("rep")
     dat = lax.axis_index("data")
@@ -144,12 +182,14 @@
         )
 
     def push(c, start, count, q):
-        ref = g.at[q, c, pl.ds(start, count)]
-        there = out.at[q, core, c, pl.ds(start, count)]
         pltpu.make_async_remote_copy(
-            src_ref=ref, dst_ref=there, send_sem=p_ss.at[q, c], recv_sem=p_rs.at[q, c], device_id=partner, device_id_type=MESH
+            src_ref=g.at[q, c, pl.ds(start, count)],
+            dst_ref=out.at[q, c, pl.ds(start, count)],
+            send_sem=p_ss.at[q, c],
+            recv_sem=p_rs.at[q, c],
+            device_id=partner,
+            device_id_type=MESH,
         ).start()
-        pltpu.make_async_copy(ref, there, o_s.at[q, c]).start()
 
     def signal(sem, dev):
         pl.semaphore_signal(sem, inc=1, device_id=dev, device_id_type=MESH)
@@ -249,15 +289,132 @@
             for direction in (0, 1):
                 signal(sem3(ag_c2, c, f, direction), sender(c, f, direction))
 
-    def load(q, par):
-        return (
-            pltpu.make_async_copy(srcs[2 * q], lr.at[par, :, pl.ds(0, cm.ff)], ld.at[par, 0]),
-            pltpu.make_async_copy(srcs[2 * q + 1], lr.at[par, :, pl.ds(cm.ff, cm.d)], ld.at[par, 1]),
-        )
+    big, small = pl.ds(0, cm.ff), pl.ds(cm.ff, cm.d)
+    loads = {
+        "a1": (a1_in, 0, big),
+        "dy": (dy_in, 0, small),
+        "h1": (h1_in, 1, small),
+        "a0": (a0_in, 0, big),
+        "x": (x_in, 1, small),
+    }
+
+    def load(name):
+        ref, par, where = loads[name]
+        return pltpu.make_async_copy(ref, lr.at[par, :, where], ld.at[list(loads).index(name)])
+
+    kt = cm.ff // KT
+    kd = cm.d // KT
+
+    def w_copy(job, k):
+        l = 1 - job // 2
+        if job % 2 == 0:
+            rows = pl.ds(pl.multiple_of(k // kd * cm.d, cm.d), cm.d)
+            src = w2.at[l, rows, pl.ds(pl.multiple_of(k % kd * KT, KT), KT)]
+        else:
+            src = w1.at[l, :, pl.ds(pl.multiple_of(k * KT, KT), KT)]
+        return pltpu.make_async_copy(src, wb.at[k % WB], w_s.at[k % WB])
+
+    def u_copy(job, n):
+        at = pl.multiple_of(n * cm.d, cm.d)
+        return pltpu.make_async_copy((u1_in if job < 2 else u0_in).at[:, pl.ds(at, cm.d)], ub, u_s)
+
+    def dot_t(a, b):
+        return lax.dot_general(a, b, (((1,), (1,)), ((), ())), preferred_element_type=F32)
+
+    rb = 16
+
+    def by_rows(fn):
+        def rows16(r, carry):
+            fn(pl.ds(pl.multiple_of(r * rb, rb), rb))
+            return carry
+
+        lax.fori_loop(0, cm.tok // rb, rows16, 0)
+
+    def clear(at):
+        acc[at, :] = jnp.zeros((rb, cm.d), F32)
+
+    def g_end(at):
+        lr[0, at, small] = (lr[0, at, small].astype(F32) + acc[at, :]).astype(BF16)
+
+    def dx_copy():
+        return pltpu.make_async_copy(lr.at[0, :, small], dx_out, d_s)
+
+    def chain(job, lo, hi):
+        odd = job % 2
+
+        def one(k, carry):
+            w_copy(0, k).wait()
+
+            @pl.when(k + WB - 1 < kt)
+            def _():
+                for j in range(NSL):
+
+                    @pl.when(job == j)
+                    def _(j=j):
+                        w_copy(j, k + WB - 1).start()
+
+            for j in (0, 2):
+
+                @pl.when((job == j) & (k % kd == 0))
+                def _(j=j):
+                    u_copy(j, k // kd).start()
+
+            @pl.when((k == 0) | ((odd == 0) & (k % kd == 0)))
+            def _():
+                by_rows(clear)
+
+            a = lr[odd, :, pl.ds(pl.multiple_of((1 - odd) * (cm.ff + k % kd * KT) + odd * k * KT, KT), KT)]
+            for n in range(kd):
+                at = pl.ds(n * KT, KT)
+                acc[:, at] = acc[:, at] + dot_t(a, wb[k % WB, n * KT : n * KT + KT, :])
+
+            @pl.when((odd == 0) & (k % kd == kd - 1))
+            def _():
+                u_copy(0, 0).wait()
+
+                def du_rows(at):
+                    v = acc[at, :] * gelu_pair(ub[at, :].astype(F32))[1]
+                    lr[1, at, pl.ds(pl.multiple_of(k // kd * cm.d, cm.d), cm.d)] = v.astype(BF16)
+
+                by_rows(du_rows)
+
+            return carry
+
+        lax.fori_loop(lo, hi, one, 0)
+        if hi == kt:
+
+            @pl.when(odd == 1)
+            def _():
+                by_rows(g_end)
+
+            for j in range(1, NSL):
+
+                @pl.when(job == j - 1)
+                def _(j=j):
+                    for k in range(WB - 1):
+                        w_copy(j, k).start()
+
+            @pl.when(job == NSL - 1)
+            def _():
+                dx_copy().start()
+
+    def chain_loads(t):
+        @pl.when(t == 1)
+        def _():
+            load("a0").start()
+
+        @pl.when(t == 2)
+        def _():
+            load("a0").wait()
+            load("x").start()
+
+        @pl.when(t == 3)
+        def _():
+            load("x").wait()
 
     jt = cm.d // TR
 
-    def compute(q, s):
+    def compute(q, lo, hi):
         par = q % 2
         odd = q % 2
 
@@ -269,9 +426,9 @@
 
         def x_copy(tau):
             return pltpu.make_async_remote_copy(
-                src_ref=stage.at[tau % 2],
+                src_ref=stage.at[tau % XB],
                 dst_ref=g.at[q, :, pl.ds(tau * cm.tu, cm.tu)],
-                send_sem=x_ss.at[tau % 2],
+                send_sem=x_ss.at[tau % XB],
                 recv_sem=x_rs.at[tau],
                 device_id=partner,
                 device_id_type=MESH,
@@ -279,29 +436,29 @@
 
         def product(tau, k, c):
             r = lr[par, :, pl.ds(cols(tau, k, c), cm.cw)]
-            return jnp.dot(lt[tau % 2], r, preferred_element_type=F32)
+            return jnp.dot(lt[tau % XB], r, preferred_element_type=F32)
 
         def tile(t, carry):
             @pl.when(t < cm.tiles)
             def _():
-                lt[t % 2] = lr[par, :, pl.ds(rows(t), TR)].T
-
-                @pl.when(t >= 2)
+                lt[t % XB] = lr[par, :, pl.ds(rows(t), TR)].T
+
+                @pl.when(t >= XB)
                 def _():
-                    x_copy(t - 2).wait_send()
+                    x_copy(t - XB).wait_send()
 
                 def colour(c, carry):
                     v = product(t, 1 - core, c).astype(BF16)
                     for u in range(cm.tu):
-                        stage[t % 2, c, u] = v[u // 2 * UR : u // 2 * UR + UR, u % 2 * UC : u % 2 * UC + UC]
+                        stage[t % XB, c, u] = v[u // 2 * UR : u // 2 * UR + UR, u % 2 * UC : u % 2 * UC + UC]
                     return carry
 
-                lax.fori_loop(0, COLOURS, colour, 0)
+                lax.fori_loop(0, COLOURS, colour, 0, unroll=True)
                 x_copy(t).start()
 
-            @pl.when(t >= 1)
-            def _():
-                tau = t - 1
+            @pl.when(t >= LAG)
+            def _():
+                tau = t - LAG
                 x_copy(tau).wait_recv()
 
                 def colour(c, carry):
@@ -312,130 +469,88 @@
                         g[q, c, tau * cm.tu + u] = w.astype(BF16)
                     return carry
 
-                lax.fori_loop(0, COLOURS, colour, 0)
+                lax.fori_loop(0, COLOURS, colour, 0, unroll=True)
 
             return carry
 
-        total = cm.tiles + 1
-        lax.fori_loop(s * total // SUB, (s + 1) * total // SUB, tile, 0)
-        if s == SUB - 1:
-            for t in (cm.tiles - 2, cm.tiles - 1):
+        lax.fori_loop(lo, hi, tile, 0)
+        if hi == cm.tiles + LAG:
+            for t in range(max(cm.tiles - XB, 0), cm.tiles):
                 x_copy(t).wait_send()
 
     barrier = pltpu.get_barrier_semaphore()
     peers = list(nbr.values()) + [partner]
     for dev in peers:
         signal(barrier, dev)
-    for cp in load(0, 0):
-        cp.start()
+    for name in ("a1", "dy", "h1"):
+        load(name).start()
+    for k in range(WB - 1):
+        w_copy(0, k).start()
+    for name in ("a1", "dy", "h1"):
+        load(name).wait()
     pl.semaphore_wait(barrier, len(peers))
 
-    def active(t, off):
-        return (t >= off) & (t < off + NSL)
-
-    def each(fn, f, q, cond=None):
-        for c in range(COLOURS):
-            fn(c, f, q)
-
-    def steps(fn, f, s, q, only=None):
+    acts = []
+
+    def act(at, rank, off, fn):
+        acts.append((at % SUB, rank, off + at // SUB, fn))
+
+    for key, off in OFF.items():
+        kind, f = key
+        step, fin, copy = (rs_step, rs_fin, rs_copy) if kind == "rs" else (ag_step, ag_fin, ag_copy)
+        c1 = rs_c1 if kind == "rs" else ag_c1
         for c in range(COLOURS):
             n = cm.n[c][f]
             for i in range(n - 1):
-                if sub_of(n, i) == s:
-                    fn(c, f, i, q)
+                at = SEND[key][n][i]
+                act(at, LATE if at < 0 else RANK[("send", *key)], off, functools.partial(step, c, f, i))
+            act(FIN[key], RANK[("fin", *key)], off, functools.partial(fin, c, f))
+            act(EARLY[key], RANK[("early", *key)], off, functools.partial(lambda c, f, copy, q: early_sends(c, f, q, copy), c, f, copy))
+
+            def credit(c, f, kind, c1, q):
+                def give():
+                    for direction in (0, 1):
+                        signal(sem3(c1, c, f, direction), sender(c, f, direction))
+
+                if kind == "ag":
+                    give()
+                elif cm.n[c][f] >= 4:
+                    pl.when(q < NSL - 1)(give)
+
+            act(CREDIT[key], RANK[("credit", *key)], off, functools.partial(credit, c, f, kind, c1))
+    for s, (lo, hi) in DW.items():
+        act(s, RANK["dw"], OFF_DW, functools.partial(lambda lo, hi, q: compute(q, lo, hi), lo, hi))
+    for s, (lo, hi) in CHAIN.items():
+        act(s, RANK["chain"], OFF_DW + 1, functools.partial(lambda lo, hi, q: chain(q, lo, hi), lo, hi))
+    acts.sort(key=lambda a: a[:3])
+    ticks = max(a[2] for a in acts) + NSL
 
     def tick(t, carry):
         for s in range(SUB):
             if s == 0:
-                for q in range(1, NSL):
-
-                    @pl.when(t + 1 == q)
-                    def _(q=q):
-                        for cp in load(q, q % 2):
-                            cp.start()
-
-                @pl.when(active(t, 0))
-                def _():
-                    for cp in load(0, t % 2):
-                        cp.wait()
-
-            for fn, f, off in ((rs_step, 0, OFF_RS[0]), (ag_step, 0, OFF_AG[0])):
-
-                @pl.when(active(t, off))
-                def _(fn=fn, f=f, off=off):
-                    steps(fn, f, s, t - off)
-
-            for fn, f, off in ((rs_step, 2, OFF_RS[2]), (ag_step, 2, OFF_AG[2]), (ag_step, 1, OFF_AG[1])):
-
-                @pl.when(active(t, off))
-                def _(fn=fn, f=f, off=off):
-                    steps(fn, f, s, t - off)
-
-            if s == 0:
-
-                @pl.when(active(t, OFF_AG[0] + 1))
-                def _():
-                    each(ag_fin, 0, t - OFF_AG[0] - 1)
-
-                @pl.when(active(t, OFF_RS[0] + 1))
-                def _():
-                    each(rs_fin, 0, t - OFF_RS[0] - 1)
-
-            @pl.when(active(t, OFF_RS[1]))
-            def _():
-                steps(rs_step, 1, s, t - OFF_RS[1])
-
-            @pl.when(active(t, 0))
-            def _():
-                compute(t, s)
-
-            if s == SUB - 2:
-                for f in range(3):
-
-                    @pl.when(active(t, OFF_RS[f]))
-                    def _(f=f):
-                        q = t - OFF_RS[f]
-                        for c in range(COLOURS):
-                            early_sends(c, f, q, rs_copy)
-                            if cm.n[c][f] >= 4:
-
-                                @pl.when(q < NSL - 1)
-                                def _(c=c):
-                                    for direction in (0, 1):
-                                        signal(sem3(rs_c1, c, f, direction), sender(c, f, direction))
-
-                    @pl.when(active(t, OFF_AG[f]))
-                    def _(f=f):
-                        for c in range(COLOURS):
-                            early_sends(c, f, t - OFF_AG[f], ag_copy)
-
-            if s == SUB - 1:
-                for f in (1, 2):
-
-                    @pl.when(active(t, OFF_RS[f]))
-                    def _(f=f):
-                        each(rs_fin, f, t - OFF_RS[f])
-
-                    @pl.when(active(t, OFF_AG[f]))
-                    def _(f=f):
-                        each(ag_fin, f, t - OFF_AG[f])
-
-                for f in range(3):
-
-                    @pl.when(active(t + 1, OFF_AG[f]))
-                    def _(f=f):
-                        for c in range(COLOURS):
-                            for direction in (0, 1):
-                                signal(sem3(ag_c1, c, f, direction), sender(c, f, direction))
+                chain_loads(t)
+            mine = [a for a in acts if a[0] == s]
+            while mine:
+                first = mine[0][2]
+                n = 0
+                while n < len(mine) and mine[n][2] == first:
+                    n += 1
+                group, mine = mine[:n], mine[n:]
+
+                @pl.when((t >= first) & (t < first + NSL))
+                def _(group=group, first=first):
+                    for _, _, _, fn in group:
+                        fn(t - first)
 
         return carry
 
-    lax.fori_loop(0, TICKS, tick, 0)
+    lax.fori_loop(0, ticks, tick, 0)
+    dx_copy().wait()
     for q in range(NSL):
         for c in range(COLOURS):
             cp = pltpu.make_async_remote_copy(
                 src_ref=g.at[q, c],
-                dst_ref=out.at[q, 1 - core, c],
+                dst_ref=out.at[q, c],
                 send_sem=p_ss.at[q, c],
                 recv_sem=p_rs.at[q, c],
                 device_id=partner,
@@ -443,7 +558,6 @@
             )
             cp.wait_send()
             cp.wait_recv()
-            pltpu.make_async_copy(g.at[q, c], out.at[q, core, c], o_s.at[q, c]).wait()
 
 
 def reduce_all(sizes, ff, d, tok, pieces):
@@ -454,46 +568,113 @@
     return pl.pallas_call(
         functools.partial(comm_kernel, cm),
         name="grad_sum",
-        out_shape=jax.ShapeDtypeStruct((NSL, 2, COLOURS, cm.units, UR, UC), BF16),
-        in_specs=[any_spec] * (2 * NSL),
-        out_specs=any_spec,
+        out_shape=(
+            pltpu.VMEM((NSL, COLOURS, cm.units, UR, UC), BF16),
+            jax.ShapeDtypeStruct((NSL, COLOURS, cm.units, UR, UC), BF16),
+            jax.ShapeDtypeStruct((tok, d), BF16),
+        ),
+        in_specs=[any_spec] * 9,
+        out_specs=(pl.BlockSpec(memory_space=pltpu.VMEM), any_spec, any_spec),
         scratch_shapes=[
-            pltpu.VMEM((NSL, COLOURS, cm.units, UR, UC), BF16),
             pltpu.VMEM((2, tok, ff + d), BF16),
-            pltpu.VMEM((2, TR, tok), BF16),
-            pltpu.VMEM((2, COLOURS, cm.tu, UR, UC), BF16),
+            pltpu.VMEM((XB, TR, tok), BF16),
+            pltpu.VMEM((XB, COLOURS, cm.tu, UR, UC), BF16),
+            pltpu.VMEM((WB, d, KT), BF16),
+            pltpu.VMEM((tok, d), BF16),
+            pltpu.VMEM((tok, d), F32),
         ]
         + cm.slot_shapes()
         + [dma((2, cm.total))] * 4
         + [reg((9, 2))] * 4
-        + [dma((2,)), dma((cm.tiles,)), dma((2, 2))]
-        + [dma((NSL, COLOURS))] * 3,
-        compiler_params=pltpu.CompilerParams(collective_id=0, has_side_effects=True, vmem_limit_bytes=66_000_000),
+        + [dma((XB,)), dma((cm.tiles,)), dma((5,))]
+        + [dma((NSL, COLOURS))] * 2
+        + [dma((WB,)), dma, dma],
+        compiler_params=pltpu.CompilerParams(collective_id=0, has_side_effects=True, vmem_limit_bytes=26_500_000),
         cost_estimate=pl.CostEstimate(flops=16 * tok * ff * d // 2, bytes_accessed=8 * ff * d, transcendentals=0),
     )(*pieces)
 
 
-def place_kernel(tu, cw, o_ref, g_ref):
-    for k in range(2):
+BUFS = 8
+AHEAD = 4
+
+
+def place_kernel(tiles, ff, d, mine_ref, o_ref, g1_ref, g2_ref, buf, in_sem, out_sem, own_sem):
+    cw = d // 2 // COLOURS
+    tr = TR // UR
+    jt = d // TR
+    total = NSL * tiles
+    core = lax.axis_index("data") % 2
+
+    def fetch(j):
+        q, tau = j // tiles, j % tiles
+        return pltpu.make_async_copy(o_ref.at[q, :, pl.ds(tau * tr, tr)], buf.at[j % BUFS], in_sem.at[j % BUFS])
+
+    def store(j, k, pieces, sem):
+        q, tau = j // tiles, j % tiles
+        l = 1 - q // 2
         for c in range(COLOURS):
-            for u in range(tu):
-                at = k * COLOURS * cw + c * cw + u % 2 * UC
-                g_ref[0, u // 2 * UR : u // 2 * UR + UR, at : at + UC] = o_ref[0, k, c, u]
-
-
-def place(o, shape, q0, where):
-    ff, d = max(shape[1:]), min(shape[1:])
-    tu, cw = TR // UR * 2, d // 2 // COLOURS
-    return pl.pallas_call(
-        functools.partial(place_kernel, tu, cw),
+            for h in range(2):
+                col = k * (d // 2) + c * cw + h * UC
+
+                @pl.when(q % 2 == 0)
+                def _():
+                    dst = g2_ref.at[l, pl.ds(tau * tr, tr), :, pl.ds(pl.multiple_of(col, UC), UC)]
+                    pltpu.make_async_copy(pieces(c, h), dst, sem).start()
+
+                @pl.when(q % 2 == 1)
+                def _():
+                    at = pl.multiple_of(tau // jt * d + col, UC)
+                    dst = g1_ref.at[l, pl.ds(tau % jt * tr, tr), :, pl.ds(at, UC)]
+                    pltpu.make_async_copy(pieces(c, h), dst, sem).start()
+
+    def drain(j):
+        b = j % BUFS
+        pltpu.make_async_copy(buf.at[b], o_ref.at[0, :, pl.ds(0, tr)], out_sem.at[b]).wait()
+
+    for j in range(AHEAD):
+        fetch(j).start()
+
+    def one(j, carry):
+        q, tau = j // tiles, j % tiles
+        store(j, core, lambda c, h: mine_ref.at[q, c, pl.ds(tau * tr, tr), h], own_sem)
+        fetch(j).wait()
+        store(j, 1 - core, lambda c, h: buf.at[j % BUFS, c, :, h], out_sem.at[j % BUFS])
+
+        @pl.when(j + AHEAD < total)
+        def _():
+            @pl.when(j + AHEAD >= BUFS)
+            def _():
+                drain(j + AHEAD - BUFS)
+
+            fetch(j + AHEAD).start()
+
+        return carry
+
+    lax.fori_loop(0, total, one, 0)
+    for j in range(total - BUFS, total):
+        drain(j)
+    pltpu.make_async_copy(mine_ref, o_ref, own_sem).wait()
+
+
+def place(mine, o, nl, ff, d):
+    tiles = ff // TR
+    any_spec = pl.BlockSpec(memory_space=pl.ANY)
+    dma = pltpu.SemaphoreType.DMA
+    shape = (NSL, COLOURS, ff // UR, 2, UR, UC)
+    g1, g2 = pl.pallas_call(
+        functools.partial(place_kernel, tiles, ff, d),
         name="place",
-        out_shape=jax.ShapeDtypeStruct(shape, BF16),
-        grid=(shape[0], ff // TR),
-        in_specs=[pl.BlockSpec((1, 2, COLOURS, tu, UR, UC), lambda l, t: (q0 - 2 * l, 0, 0, t, 0, 0))],
-        out_specs=pl.BlockSpec((1, TR, d), where),
-        compiler_params=pltpu.CompilerParams(dimension_semantics=("arbitrary", "arbitrary")),
-        cost_estimate=pl.CostEstimate(flops=0, bytes_accessed=8 * ff * d, transcendentals=0),
-    )(o)
+        out_shape=(
+            jax.ShapeDtypeStruct((nl, d // UR, UR, ff), BF16),
+            jax.ShapeDtypeStruct((nl, ff // UR, UR, d), BF16),
+        ),
+        in_specs=[any_spec, any_spec],
+        out_specs=(any_spec, any_spec),
+        scratch_shapes=[pltpu.VMEM((BUFS, COLOURS, TR // UR, 2, UR, UC), BF16), dma((BUFS,)), dma((BUFS,)), dma],
+        compiler_params=pltpu.CompilerParams(vmem_limit_bytes=16_000_000),
+        cost_estimate=pl.CostEstimate(flops=0, bytes_accessed=16 * ff * d, transcendentals=0),
+    )(pltpu.with_memory_space_constraint(mine.reshape(shape), pltpu.VMEM), o.reshape(shape))
+    return g1.reshape(nl, d, ff), g2.reshape(nl, ff, d)
 
 
 def solution(mesh, sizes=None):
@@ -519,16 +700,8 @@
             acts.append(act)
             if l + 1 < nl:
                 h = (h.astype(F32) + mm(act, w2[l])).astype(BF16)
-        pieces = []
-        for l in reversed(range(nl)):
-            da = mm(g, w2[l].T)
-            du = (da * gelu_pair(us[l].astype(F32))[1]).astype(BF16)
-            pieces += [acts[l], g, du, hs[l]]
-            g = (g.astype(F32) + mm(du, w1[l].T)).astype(BF16)
-        o = reduce_all(sizes, ff, nd, tok, pieces)
-        jt = nd // TR
-        g1 = place(o, w1.shape, 3, lambda l, t: (l, t % jt, t // jt))
-        g2 = place(o, w2.shape, 2, lambda l, t: (l, t, 0))
-        return g1, g2, g.reshape(x.shape)
+        mine, o, dx = reduce_all(sizes, ff, nd, tok, [hs[0], g, hs[1], acts[1], acts[0], us[1], us[0], w1, w2])
+        g1, g2 = place(mine, o, nl, ff, nd)
+        return g1, g2, dx.reshape(x.shape)
 
     return jax.shard_map(local, mesh=mesh, in_specs=(P(), P(), P(AXES), P(AXES)), out_specs=(P(), P(), P(AXES)), check_vma=False)

time: 516 us -> 393 us (0.76)
  Pallas kernels: 438 us -> 360 us
  matrix products: 75.3 us -> 30.6 us
    dot_general x7 -> x3, matrix products: 75.3 us -> 30.6 us  [mm(): return jnp.dot(a, b, preferred_element_type=F32)]
    pallas_call x1, Pallas kernels: 361 us -> 322 us  [reduce_all(): pl.pallas_call(functools.partial(comm_kernel, cm), name='grad_sum', out_s...]
    pallas_call x2 -> x1, Pallas kernels: 77 us -> 37.9 us  [place(): pl.pallas_call(functools.partial(place_kernel, tiles, ff, d), name='place...]
where the time goes in v2:
time: 393 us; the launch traced here: 392 us
  Pallas kernels  360 us (92%)
  matrix products  30.6 us (8%)
    pallas_call x1, Pallas kernels, reduce_all(): pl.pallas_call(functools.partial(comm_kernel, cm), name='grad_sum', out_s...  322 us
    pallas_call x1, Pallas kernels, place(): pl.pallas_call(functools.partial(place_kernel, tiles, ff, d), name='place...  37.9 us
    dot_general x3, matrix products, mm(): return jnp.dot(a, b, preferred_element_type=F32)  30.6 us

profile of v2, /device:TPU:1, one launch (start us, length us, event | category | flops | bytes accessed | tf_op | source)
XLA Modules:
  0.0 391.7 jit_solution(12750376339869933010)
XLA Ops:
  0.6 0.0 copy-start.1
  0.6 10.2 %fusion.16 = (bf16[192,6144]{1,0:T(8,128)(2,1)}, bf16[192,6144]{1,0:T(8,128)(2,1)S(1)}) fusion(bf16[192,1536]{1,0:T(8,128)(2,1)} %bitcast.34, bf16[2,1536,6144]{2,1,0:T(8,128)(2,1)} %refs_7_.1), kind=kOutput, calls=%fused_computation.22 | convolution fusion | flops 3636854784 | bytes 24182784 | tf_op jit(solution)/shard_map/dot_general | solution.py:690
  10.9 0.0 copy-start
  10.9 0.0 copy-done.1
  10.9 9.7 %fusion.28.refs_2_ = bf16[192,1536]{1,0:T(8,128)(2,1)S(1)} fusion(bf16[2,6144,1536]{2,1,0:T(8,128)(2,1)} %refs_8_.1, bf16[192,1536]{1,0:T(8,128)(2,1)S(1)} %bitcast.36, bf16[192,6144]{1,0:T(8,128)(2,1)S(1)} %get-tuple-element.19.refs_6_), kind=kOutput, calls=%fused_computation.32 | convolution fusion | flops 3636559872 | bytes 22413312 | tf_op jit(solution)/shard_map/dot_general | solution.py:690
  20.6 0.0 copy-done
  20.6 0.0 copy-start.2
  20.6 10.7 %fusion.21 = (bf16[192,6144]{1,0:T(8,128)(2,1)}, bf16[192,6144]{1,0:T(8,128)(2,1)}) fusion(bf16[192,1536]{1,0:T(8,128)(2,1)S(1)} %fusion.28.refs_2_, bf16[2,1536,6144]{2,1,0:T(8,128)(2,1)} %refs_7_.1), kind=kOutput, calls=%fused_computation.27 | convolution fusion | flops 3636854784 | bytes 24182784 | tf_op jit(solution)/shard_map/dot_general | solution.py:690
  31.3 0.0 copy-done.2
  31.3 321.6 %grad_sum.1 = (bf16[4,3,256,48,128]{4,3,2,1,0:T(8,128)(2,1)S(1)}, bf16[4,3,256,48,128]{4,3,2,1,0:T(8,128)(2,1)}, bf16[192,1536]{1,0:T(8,128)(2,1)}) custom-call(bf16[192,1536]{1,0:T(8,128)(2,1)} %bitcast.35, bf16[192,1536]{1,0:T(8,128)(2,1)} %bitcast.37, bf16[192,1536]{1,0:T(8,128)(2,1)} %copy-done.2, bf16[192,6144]{1,0:T(8,128)(2,1)} %get-tuple-element.16.refs_3_, ...), custom_call_target="tpu_custom_call" | custom-call | flops 14495514624 | bytes 75497472 | tf_op jit(solution)/shard_map/grad_sum/pallas_call | solution.py:568
  353.0 0.0 copy-start.3
  353.0 37.9 %place.1 = (bf16[2,32,48,6144]{3,2,1,0:T(8,128)(2,1)}, bf16[2,128,48,1536]{3,2,1,0:T(8,128)(2,1)}) custom-call(bf16[4,3,128,2,48,128]{5,4,3,2,1,0:T(8,128)(2,1)S(1)} %bitcast.32, bf16[4,3,128,2,48,128]{5,4,3,2,1,0:T(8,128)(2,1)} %bitcast.33), custom_call_target="tpu_custom_call" | custom-call | bytes 150994944 | tf_op jit(solution)/shard_map/place/pallas_call | solution.py:664
  390.9 0.0 copy-done.3
  390.9 0.8 copy.9
Async XLA Ops:
  0.6 10.2 %copy-start.1 = (bf16[3,1,64,1536]{3,2,1,0:T(8,128)(2,1)S(1)}, bf16[3,1,64,1536]{3,2,1,0:T(8,128)(2,1)}, u32[]{:S(2)}) copy-start(bf16[3,1,64,1536]{3,2,1,0:T(8,128)(2,1)} %param.6) | copy-start | bytes 1769476
  10.9 9.7 %copy-start = (bf16[192,6144]{1,0:T(8,128)(2,1)}, bf16[192,6144]{1,0:T(8,128)(2,1)S(1)}, u32[]{:S(2)}) copy-start(bf16[192,6144]{1,0:T(8,128)(2,1)S(1)} %get-tuple-element.19.refs_6_) | copy-start | bytes 7077892
  20.6 10.7 %copy-start.2 = (bf16[192,1536]{1,0:T(8,128)(2,1)}, bf16[192,1536]{1,0:T(8,128)(2,1)S(1)}, u32[]{:S(2)}) copy-start(bf16[192,1536]{1,0:T(8,128)(2,1)S(1)} %fusion.28.refs_2_) | copy-start | bytes 1769476
  353.0 38.0 %copy-start.3 = (bf16[192,1536]{1,0:T(8,128)(2,1)S(1)}, bf16[192,1536]{1,0:T(8,128)(2,1)}, u32[]{:S(2)}) copy-start(bf16[192,1536]{1,0:T(8,128)(2,1)} %get-tuple-element.12) | copy-start | bytes 1769476

commit v3 on v2

--- a/solution.py
+++ b/solution.py
@@ -18,53 +18,54 @@
 TR = 384
 COLOURS = 3
 ORDERS = (("x", "y", "z"), ("y", "x", "z"), ("z", "x", "y"))
+ODD_ORDERS = (("x", "y", "z"), ("y", "x", "z"), ("z", "y", "x"))
 SUB = 8
 NSL = 4
 OFF_DW = 0
 OFF = {("rs", 0): 1, ("rs", 1): 2, ("rs", 2): 3, ("ag", 2): 4, ("ag", 1): 5, ("ag", 0): 6}
 SEND = {
-    ("rs", 0): {8: (0, 1, 2, 2, 3, 6, 7), 4: (0, 2, 4), 2: (1,)},
-    ("rs", 1): {8: (-1, 6, 11, 9, 8, 6, 10), 4: (0, 0, 2), 2: (1,)},
-    ("rs", 2): {8: (-1, 0, 1, 1, 2, 2, 5), 4: (1, 3, 4), 2: (1,)},
-    ("ag", 2): {8: (0, 1, 2, 2, 3, 4, 5), 4: (0, 0, 4), 2: (1,)},
-    ("ag", 1): {8: (1, -1, -2, 8, 2, 5, 8), 4: (-1, 0, 1), 2: (1,)},
-    ("ag", 0): {8: (0, 0, 1, 2, 3, 6, 6), 4: (-2, 2, 3), 2: (1,)},
+    ("rs", 0): {8: (0, 1, 2, 2, 3, 6, 7), 4: (0, 2, 6), 2: (1,)},
+    ("rs", 1): {8: (-4, 7, 14, 10, 10, 5, 9), 4: (0, 3, 3), 2: (1,)},
+    ("rs", 2): {8: (-1, -1, 1, 1, 2, 2, 6), 4: (-1, 2, 2), 2: (1,)},
+    ("ag", 2): {8: (-1, 1, 2, 2, 4, 5, 6), 4: (0, 0, 3), 2: (1,)},
+    ("ag", 1): {8: (3, 0, -3, 7, 4, 9, 6), 4: (-1, -1, 3), 2: (1,)},
+    ("ag", 0): {8: (-2, 0, 1, 1, 2, 4, 6), 4: (-2, 1, 3), 2: (1,)},
 }
-FIN = {("rs", 0): 8, ("rs", 1): 7, ("rs", 2): 7, ("ag", 2): 7, ("ag", 1): 5, ("ag", 0): 8}
-EARLY = {("rs", 0): 6, ("rs", 1): 7, ("rs", 2): 7, ("ag", 2): 7, ("ag", 1): 3, ("ag", 0): 4}
-CREDIT = {("rs", 0): 7, ("rs", 1): 5, ("rs", 2): 6, ("ag", 2): -1, ("ag", 1): -4, ("ag", 0): -2}
+FIN = {("rs", 0): 8, ("rs", 1): 7, ("rs", 2): 6, ("ag", 2): 7, ("ag", 1): 6, ("ag", 0): 8}
+EARLY = {("rs", 0): 7, ("rs", 1): 7, ("rs", 2): 6, ("ag", 2): 5, ("ag", 1): 4, ("ag", 0): 5}
+CREDIT = {("rs", 0): 7, ("rs", 1): 7, ("rs", 2): 6, ("ag", 2): -2, ("ag", 1): -5, ("ag", 0): -2}
 RANK = {
     "load": 0,
-    ("send", "ag", 1): 1,
-    ("early", "ag", 2): 2,
-    ("send", "ag", 2): 3,
-    ("send", "rs", 2): 4,
-    ("send", "rs", 0): 5,
-    ("send", "ag", 0): 6,
-    ("fin", "ag", 2): 7,
-    ("early", "rs", 1): 8,
-    "chain": 9,
-    ("fin", "rs", 1): 10,
-    ("fin", "ag", 1): 11,
-    ("credit", "ag", 1): 12,
-    ("early", "ag", 1): 13,
-    ("early", "ag", 0): 14,
-    ("credit", "ag", 0): 15,
-    ("fin", "rs", 0): 16,
-    ("fin", "ag", 0): 17,
+    ("fin", "rs", 1): 1,
+    ("send", "rs", 2): 2,
+    ("send", "rs", 0): 3,
+    ("send", "ag", 1): 4,
+    ("early", "ag", 2): 5,
+    ("fin", "ag", 1): 6,
+    ("send", "ag", 2): 7,
+    ("fin", "ag", 2): 8,
+    ("early", "ag", 1): 9,
+    "chain": 10,
+    ("send", "ag", 0): 11,
+    ("credit", "rs", 1): 12,
+    ("credit", "ag", 1): 13,
+    ("credit", "ag", 0): 14,
+    ("fin", "rs", 0): 15,
+    ("credit", "rs", 0): 16,
+    ("early", "rs", 1): 17,
     ("early", "rs", 2): 18,
-    ("credit", "rs", 1): 19,
-    ("credit", "rs", 0): 20,
-    ("fin", "rs", 2): 21,
-    "dw": 22,
-    ("send", "rs", 1): 24,
-    ("credit", "rs", 2): 25,
-    ("early", "rs", 0): 26,
+    ("credit", "rs", 2): 19,
+    ("early", "ag", 0): 20,
+    ("early", "rs", 0): 21,
+    ("fin", "ag", 0): 22,
+    ("send", "rs", 1): 23,
+    "dw": 24,
+    ("fin", "rs", 2): 26,
     ("credit", "ag", 2): 27,
 }
-LATE = 23
-CHAIN = {0: (0, 5), 1: (5, 12)}
-DW = {1: (0, 1), 2: (1, 7), 3: (7, 9), 5: (9, 11), 6: (11, 16), 7: (16, 18)}
+LATE = 25
+CHAIN = {0: (0, 7), 1: (7, 12)}
+DW = {1: (0, 2), 2: (2, 10), 4: (10, 12), 6: (12, 17), 7: (17, 18)}
 KT = 512
 WB = 3
 XB = 3
@@ -129,55 +130,61 @@
     nbr = {(a, s): device(a, s) for a in ("x", "y", "z") for s in (1, -1)}
     partner = {"rep": rep, "data": pos["x"] * 2 + (1 - core)}
 
-    def neighbour(c, f, direction):
-        return nbr[(ORDERS[c][f], 1 if direction == 0 else -1)]
-
-    def sender(c, f, direction):
-        return nbr[(ORDERS[c][f], -1 if direction == 0 else 1)]
-
-    bases = []
-    for c in range(COLOURS):
-        b, bs = 0, []
-        for f in range(3):
-            bs.append(b)
-            b = b + pos[ORDERS[c][f]] * cm.stride[c][f]
-        bases.append(bs)
-
-    def region(c, f, step, half):
+    def either(q, even, odd):
+        return even * (1 - q % 2) + odd * (q % 2)
+
+    def beside(c, f, step, q):
+        a, b = nbr[(ORDERS[c][f], step)], nbr[(ODD_ORDERS[c][f], step)]
+        return a if a is b else {k: either(q, a[k], b[k]) for k in a}
+
+    def neighbour(c, f, direction, q):
+        return beside(c, f, 1 if direction == 0 else -1, q)
+
+    def sender(c, f, direction, q):
+        return beside(c, f, -1 if direction == 0 else 1, q)
+
+    def place_on(c, f, q):
+        a, b = ORDERS[c][f], ODD_ORDERS[c][f]
+        return pos[a] if a == b else either(q, pos[a], pos[b])
+
+    def region(c, f, step, half, q):
         n, s = cm.n[c][f], cm.stride[c][f]
-        owner = (pos[ORDERS[c][f]] + step + n) % n
-        return bases[c][f] + owner * s + half * (s // 2)
-
-    def rs_region(c, f, direction, i):
+        owner = (place_on(c, f, q) + step + n) % n
+        at = owner * s + half * (s // 2)
+        for e in range(f):
+            at = at + place_on(c, e, q) * cm.stride[c][e]
+        return at
+
+    def rs_region(c, f, direction, i, q):
         k = cm.n[c][f] // 2 - (i + 1) // 2
-        return region(c, f, k if direction == 0 else -k, half_of(direction, i))
-
-    def ag_region(c, f, direction, i):
+        return region(c, f, k if direction == 0 else -k, half_of(direction, i), q)
+
+    def ag_region(c, f, direction, i, q):
         k = i // 2
-        return region(c, f, -k if direction == 0 else k, half_of(direction, i))
+        return region(c, f, -k if direction == 0 else k, half_of(direction, i), q)
 
     def rs_copy(c, f, direction, i, q):
         h = cm.stride[c][f] // 2
         j = cm.off[c][f] + i
         return pltpu.make_async_remote_copy(
-            src_ref=g.at[q, c, pl.ds(rs_region(c, f, direction, i), h)],
+            src_ref=g.at[q, c, pl.ds(rs_region(c, f, direction, i, q), h)],
             dst_ref=slots[3 * c + f].at[direction, i],
             send_sem=rs_ss.at[direction, j],
             recv_sem=rs_rs.at[direction, j],
-            device_id=neighbour(c, f, direction),
+            device_id=neighbour(c, f, direction, q),
             device_id_type=MESH,
         )
 
     def ag_copy(c, f, direction, i, q):
         h = cm.stride[c][f] // 2
         j = cm.off[c][f] + i
-        ref = g.at[q, c, pl.ds(ag_region(c, f, direction, i), h)]
+        ref = g.at[q, c, pl.ds(ag_region(c, f, direction, i, q), h)]
         return pltpu.make_async_remote_copy(
             src_ref=ref,
             dst_ref=ref,
             send_sem=ag_ss.at[direction, j],
             recv_sem=ag_rs.at[direction, j],
-            device_id=neighbour(c, f, direction),
+            device_id=neighbour(c, f, direction, q),
             device_id_type=MESH,
         )
 
@@ -194,8 +201,8 @@
     def signal(sem, dev):
         pl.semaphore_signal(sem, inc=1, device_id=dev, device_id_type=MESH)
 
-    def sem3(ref, c, f, direction):
-        return ref.at[3 * c + f, direction]
+    def sem3(ref, c, f, direction, q):
+        return ref.at[3 * c + f, direction, q % 2]
 
     def add_units(c, start, h, parts, q):
         b = min(8, h)
@@ -218,35 +225,35 @@
         for direction in (0, 1):
             if i >= 2:
                 rs_copy(c, f, direction, i - 2, q).wait_recv()
-                add_units(c, rs_region(c, f, direction, i), h, [(slots[3 * c + f], direction, i - 2)], q)
+                add_units(c, rs_region(c, f, direction, i, q), h, [(slots[3 * c + f], direction, i - 2)], q)
 
             @pl.when(q >= 1)
             def _():
                 if i == 0 and n >= 4:
-                    pl.semaphore_wait(sem3(rs_c1, c, f, direction), 1)
+                    pl.semaphore_wait(sem3(rs_c1, c, f, direction, q), 1)
                 if i == max(n - 3, 0):
-                    pl.semaphore_wait(sem3(rs_c2, c, f, direction), 1)
+                    pl.semaphore_wait(sem3(rs_c2, c, f, direction, q), 1)
 
             rs_copy(c, f, direction, i, q).start()
 
     def ag_step(c, f, i, q):
         n, h = cm.n[c][f], cm.stride[c][f] // 2
         if f == 0 and i == 0:
-            push(c, region(c, f, 0, 0), 2 * h, q)
+            push(c, region(c, f, 0, 0, q), 2 * h, q)
         for direction in (0, 1):
             if i >= 2:
                 ag_copy(c, f, direction, i - 2, q).wait_recv()
             if i == 0:
-                pl.semaphore_wait(sem3(ag_c1, c, f, direction), 1)
+                pl.semaphore_wait(sem3(ag_c1, c, f, direction, q), 1)
             if i == max(n - 3, 0):
 
                 @pl.when(q >= 1)
                 def _():
-                    pl.semaphore_wait(sem3(ag_c2, c, f, direction), 1)
+                    pl.semaphore_wait(sem3(ag_c2, c, f, direction, q), 1)
 
             ag_copy(c, f, direction, i, q).start()
             if f == 0 and i >= 2:
-                push(c, ag_region(c, f, direction, i), h, q)
+                push(c, ag_region(c, f, direction, i, q), h, q)
 
     def early_sends(c, f, q, copy):
         for i in range(min(2, cm.n[c][f] - 1)):
@@ -266,13 +273,13 @@
                 rs_copy(c, f, direction, m, q).wait_recv()
                 parts[half_of(direction, m)].append((slots[3 * c + f], direction, m))
         for half in (0, 1):
-            add_units(c, region(c, f, 0, half), h, parts[half], q)
+            add_units(c, region(c, f, 0, half, q), h, parts[half], q)
         late_sends(c, f, q, rs_copy)
 
         @pl.when(q < NSL - 1)
         def _():
             for direction in (0, 1):
-                signal(sem3(rs_c2, c, f, direction), sender(c, f, direction))
+                signal(sem3(rs_c2, c, f, direction, q + 1), sender(c, f, direction, q + 1))
 
     def ag_fin(c, f, q):
         n, h = cm.n[c][f], cm.stride[c][f] // 2
@@ -281,13 +288,13 @@
                 ag_copy(c, f, direction, m, q).wait_recv()
                 if f == 0:
                     k = m // 2 + 1
-                    push(c, region(c, f, -k if direction == 0 else k, half_of(direction, m)), h, q)
+                    push(c, region(c, f, -k if direction == 0 else k, half_of(direction, m), q), h, q)
         late_sends(c, f, q, ag_copy)
 
         @pl.when(q < NSL - 1)
         def _():
             for direction in (0, 1):
-                signal(sem3(ag_c2, c, f, direction), sender(c, f, direction))
+                signal(sem3(ag_c2, c, f, direction, q + 1), sender(c, f, direction, q + 1))
 
     big, small = pl.ds(0, cm.ff), pl.ds(cm.ff, cm.d)
     loads = {
@@ -510,7 +517,8 @@
             def credit(c, f, kind, c1, q):
                 def give():
                     for direction in (0, 1):
-                        signal(sem3(c1, c, f, direction), sender(c, f, direction))
+                        r = q if kind == "ag" else q + 1
+                        signal(sem3(c1, c, f, direction, r), sender(c, f, direction, r))
 
                 if kind == "ag":
                     give()
@@ -585,7 +593,7 @@
         ]
         + cm.slot_shapes()
         + [dma((2, cm.total))] * 4
-        + [reg((9, 2))] * 4
+        + [reg((9, 2, 2))] * 4
         + [dma((XB,)), dma((cm.tiles,)), dma((5,))]
         + [dma((NSL, COLOURS))] * 2
         + [dma((WB,)), dma, dma],
@@ -594,8 +602,8 @@
     )(*pieces)
 
 
-BUFS = 8
-AHEAD = 4
+BUFS = 16
+AHEAD = 12
 
 
 def place_kernel(tiles, ff, d, mine_ref, o_ref, g1_ref, g2_ref, buf, in_sem, out_sem, own_sem):

time: 393 us -> 386 us (0.982)
  Pallas kernels: 360 us -> 353 us
    pallas_call x1, Pallas kernels: 322 us -> 317 us  [reduce_all(): pl.pallas_call(functools.partial(comm_kernel, cm), name='grad_sum', out_s...]
where the time goes in v3:
time: 386 us
  Pallas kernels  353 us (91%)
  matrix products  30.6 us (8%)
    pallas_call x1, Pallas kernels, reduce_all(): pl.pallas_call(functools.partial(comm_kernel, cm), name='grad_sum', out_s...  317 us
    pallas_call x1, Pallas kernels, place(): pl.pallas_call(functools.partial(place_kernel, tiles, ff, d), name='place...  36.2 us
    dot_general x3, matrix products, mm(): return jnp.dot(a, b, preferred_element_type=F32)  30.6 us

profile of v3, /device:TPU:1, one launch (start us, length us, event | category | flops | bytes accessed | tf_op | source)
XLA Modules:
  0.0 385.5 jit_solution(9319393218717092669)
XLA Ops:
  0.6 0.0 copy-start.1
  0.6 10.2 %fusion.16 = (bf16[192,6144]{1,0:T(8,128)(2,1)}, bf16[192,6144]{1,0:T(8,128)(2,1)S(1)}) fusion(bf16[192,1536]{1,0:T(8,128)(2,1)} %bitcast.34, bf16[2,1536,6144]{2,1,0:T(8,128)(2,1)} %refs_7_.1), kind=kOutput, calls=%fused_computation.22 | convolution fusion | flops 3636854784 | bytes 24182784 | tf_op jit(solution)/shard_map/dot_general | solution.py:698
  10.9 0.0 copy-start
  10.9 0.0 copy-done.1
  10.9 9.7 %fusion.28.refs_2_ = bf16[192,1536]{1,0:T(8,128)(2,1)S(1)} fusion(bf16[2,6144,1536]{2,1,0:T(8,128)(2,1)} %refs_8_.1, bf16[192,1536]{1,0:T(8,128)(2,1)S(1)} %bitcast.36, bf16[192,6144]{1,0:T(8,128)(2,1)S(1)} %get-tuple-element.19.refs_6_), kind=kOutput, calls=%fused_computation.32 | convolution fusion | flops 3636559872 | bytes 22413312 | tf_op jit(solution)/shard_map/dot_general | solution.py:698
  20.6 0.0 copy-done
  20.6 0.0 copy-start.2
  20.6 10.7 %fusion.21 = (bf16[192,6144]{1,0:T(8,128)(2,1)}, bf16[192,6144]{1,0:T(8,128)(2,1)}) fusion(bf16[192,1536]{1,0:T(8,128)(2,1)S(1)} %fusion.28.refs_2_, bf16[2,1536,6144]{2,1,0:T(8,128)(2,1)} %refs_7_.1), kind=kOutput, calls=%fused_computation.27 | convolution fusion | flops 3636854784 | bytes 24182784 | tf_op jit(solution)/shard_map/dot_general | solution.py:698
  31.3 0.0 copy-done.2
  31.3 317.2 %grad_sum.1 = (bf16[4,3,256,48,128]{4,3,2,1,0:T(8,128)(2,1)S(1)}, bf16[4,3,256,48,128]{4,3,2,1,0:T(8,128)(2,1)}, bf16[192,1536]{1,0:T(8,128)(2,1)}) custom-call(bf16[192,1536]{1,0:T(8,128)(2,1)} %bitcast.35, bf16[192,1536]{1,0:T(8,128)(2,1)} %bitcast.37, bf16[192,1536]{1,0:T(8,128)(2,1)} %copy-done.2, bf16[192,6144]{1,0:T(8,128)(2,1)} %get-tuple-element.16.refs_3_, ...), custom_call_target="tpu_custom_call" | custom-call | flops 14495514624 | bytes 75497472 | tf_op jit(solution)/shard_map/grad_sum/pallas_call | solution.py:576
  348.5 0.0 copy-start.3
  348.5 36.2 %place.1 = (bf16[2,32,48,6144]{3,2,1,0:T(8,128)(2,1)}, bf16[2,128,48,1536]{3,2,1,0:T(8,128)(2,1)}) custom-call(bf16[4,3,128,2,48,128]{5,4,3,2,1,0:T(8,128)(2,1)S(1)} %bitcast.32, bf16[4,3,128,2,48,128]{5,4,3,2,1,0:T(8,128)(2,1)} %bitcast.33), custom_call_target="tpu_custom_call" | custom-call | bytes 150994944 | tf_op jit(solution)/shard_map/place/pallas_call | solution.py:672
  384.7 0.0 copy-done.3
  384.7 0.8 copy.9
Async XLA Ops:
  0.6 10.2 %copy-start.1 = (bf16[3,1,64,1536]{3,2,1,0:T(8,128)(2,1)S(1)}, bf16[3,1,64,1536]{3,2,1,0:T(8,128)(2,1)}, u32[]{:S(2)}) copy-start(bf16[3,1,64,1536]{3,2,1,0:T(8,128)(2,1)} %param.6) | copy-start | bytes 1769476
  10.9 9.7 %copy-start = (bf16[192,6144]{1,0:T(8,128)(2,1)}, bf16[192,6144]{1,0:T(8,128)(2,1)S(1)}, u32[]{:S(2)}) copy-start(bf16[192,6144]{1,0:T(8,128)(2,1)S(1)} %get-tuple-element.19.refs_6_) | copy-start | bytes 7077892
  20.6 10.7 %copy-start.2 = (bf16[192,1536]{1,0:T(8,128)(2,1)}, bf16[192,1536]{1,0:T(8,128)(2,1)S(1)}, u32[]{:S(2)}) copy-start(bf16[192,1536]{1,0:T(8,128)(2,1)S(1)} %fusion.28.refs_2_) | copy-start | bytes 1769476
  348.5 36.3 %copy-start.3 = (bf16[192,1536]{1,0:T(8,128)(2,1)S(1)}, bf16[192,1536]{1,0:T(8,128)(2,1)}, u32[]{:S(2)}) copy-start(bf16[192,1536]{1,0:T(8,128)(2,1)} %get-tuple-element.12) | copy-start | bytes 1769476
